TPU v7x, 256 devices: a whole 4x4x8 slice. The times are simulated.
256 devices in a mesh: half: 2 (over core), row: 16 (over x, y), col: 8 (over z).
Axes of the slice: x: 4, y: 4, z: 8, core: 2. Of those that a mesh axis runs over, the one named last changes fastest.
Arguments:
- particles: bfloat16 [512, 2, 64, 4096], P(('half', 'row', 'col')), may hold values from -9 to 9
- orient_bin: int32 [512], P(('half', 'row', 'col')), may hold values from 0 to 15
- tilt_slope: int32 [512, 2], P(('half', 'row', 'col')), may hold values from 12 to 40
- interp_table: bfloat16 [16, 3, 64, 64], replicated, may hold values from 0 to 1.6, as said below
Outputs:
- half_maps: float32 [2, 2, 64, 4096], P('half', None, 'row', 'col')
- shell_power: float32 [2, 29], replicated
- shell_correlation: float32 [2, 29], P('half')
Inputs may be any that keep to these rules, and one draw needn't show every extreme that they name: `interp_table`: nonnegative entries.
All inputs are finite; a program needn't handle non-finite values.
Results may differ from a plain program's by a relative error of at most 0.00063.
Values sent between devices are 32-bit elements; how exact they have to be, the bound alone decides.
A program may use at most 64 MiB of HBM per device.

v0:
```python
import functools

import jax
import jax.numpy as jnp
from jax import lax
from jax.sharding import Mesh
from jax.sharding import PartitionSpec as P

SHELLS = 29
ROW = ("row_0", "row_1")
ROW_COL = ("row_0", "row_1", "col")
HALF_ROW_COL = ("half", "row_0", "row_1", "col")


def split_up(x, dim, size):
    before, after = (x.shape[:dim], x.shape[dim + 1 :])
    return jnp.moveaxis(x.reshape(*before, size, -1, *after), dim, 0)


def summed_on_arrival(x, axis, dim):
    size = lax.axis_size(axis)
    parts = lax.all_to_all(split_up(x, dim, size), axis, 0, 0, tiled=True)
    return jnp.sum(parts, axis=0)


def partner_2(value, axis, distance):
    mask = 2**distance
    pairs = [(source, source ^ mask) for source in range(lax.axis_size(axis))]
    return lax.ppermute(value, axis, pairs)


def one_axis_at_a_time(x, axes):
    return functools.reduce(lax.psum, axes, x)


def wedge_mask(tilt_limits, grid_size):
    centre = grid_size // 2
    wave_first = (jnp.arange(grid_size, dtype=jnp.int32) - centre)[:, None]
    wave_third = (jnp.arange(grid_size * grid_size, dtype=jnp.int32) % grid_size - centre)[None, :]
    tilt_limit = jnp.where(wave_first * wave_third >= 0, tilt_limits[0], tilt_limits[1])
    inside = 16 * jnp.abs(wave_third) <= tilt_limit * jnp.abs(wave_first)
    return inside.astype(jnp.float32)


def interpolate(stacked, kernels, grid_size):
    components = stacked.shape[0]
    along_first = jnp.einsum(
        "ax,cxm->cam", kernels[0], stacked, preferred_element_type=jnp.float32
    ).astype(jnp.bfloat16)
    along_first = along_first.reshape(components, grid_size, grid_size, grid_size)
    along_second = jnp.einsum(
        "by,cayz->cabz", kernels[1], along_first, preferred_element_type=jnp.float32
    ).astype(jnp.bfloat16)
    along_third = jnp.einsum(
        "dz,cabz->cabd", kernels[2], along_second, preferred_element_type=jnp.float32
    )
    return along_third.reshape(components, grid_size, grid_size * grid_size)


def shell_table(first_index, plane_index, grid_size, shells):
    centre = grid_size // 2
    wave_first = first_index - centre
    wave_second = plane_index // grid_size - centre
    wave_third = plane_index % grid_size - centre
    radius_sq = (
        wave_first * wave_first + wave_second * wave_second + wave_third * wave_third
    ).reshape(-1)
    bounds = jnp.arange(4, centre, dtype=jnp.int32)
    shell_index = jnp.sum(
        (radius_sq[:, None] >= (bounds * bounds)[None, :]).astype(jnp.int32), axis=1
    )
    within = radius_sq < centre * centre
    onehot = (shell_index[:, None] == jnp.arange(shells, dtype=jnp.int32)[None, :]) & within[
        :, None
    ]
    return onehot.astype(jnp.float32)


def spread_slabs(volume):
    slabs = summed_on_arrival(volume, ROW, 1)
    return summed_on_arrival(slabs, "col", 2)


def local(particles, orient_bin, tilt_slope, interp_table):
    grid_size = particles.shape[2]
    particle_count = particles.shape[0]
    rows_local = grid_size // lax.axis_size(ROW)
    cols_local = grid_size * grid_size // lax.axis_size("col")
    components = 3

    def insert_one(particle, partial_value):
        volume_data = lax.dynamic_index_in_dim(particles, particle, 0, keepdims=False)
        bin_row = lax.dynamic_index_in_dim(orient_bin, particle, 0, keepdims=False)
        tilt_limits = lax.dynamic_index_in_dim(tilt_slope, particle, 0, keepdims=False)
        weight = wedge_mask(tilt_limits, grid_size)
        stacked = jnp.stack([volume_data[0] * weight, volume_data[1] * weight, weight]).astype(
            jnp.bfloat16
        )
        kernels = lax.dynamic_index_in_dim(interp_table, bin_row, 0, keepdims=False)
        return partial_value + interpolate(stacked, kernels, grid_size)

    partial_value = jnp.zeros((components, grid_size, grid_size * grid_size), jnp.float32)
    partial_value = lax.fori_loop(0, particle_count, insert_one, partial_value)
    sums = spread_slabs(partial_value)
    weight_sum = sums[2]
    half_maps = (sums[:2] / (weight_sum[None] + 1.0))[None]
    partner = partner_2(half_maps, "half", 0)
    on_first = lax.axis_index("half") == 0
    map_first = jnp.where(on_first, half_maps, partner)[0]
    map_second = jnp.where(on_first, partner, half_maps)[0]
    cross_term = (map_first[0] * map_second[0] + map_first[1] * map_second[1]).reshape(-1)
    power_first = (map_first[0] * map_first[0] + map_first[1] * map_first[1]).reshape(-1)
    power_second = (map_second[0] * map_second[0] + map_second[1] * map_second[1]).reshape(-1)
    products = jnp.stack([cross_term, power_first, power_second])
    first_index = (
        lax.axis_index(ROW) * rows_local + jnp.arange(rows_local, dtype=jnp.int32)[:, None]
    )
    plane_index = (
        lax.axis_index("col") * cols_local + jnp.arange(cols_local, dtype=jnp.int32)[None, :]
    )
    onehot = shell_table(first_index, plane_index, grid_size, SHELLS)
    spectra = jnp.dot(products, onehot, precision=lax.Precision.HIGHEST)
    counts = jnp.sum(onehot, axis=0)
    spectra, counts = (one_axis_at_a_time(spectra, ROW_COL), one_axis_at_a_time(counts, ROW_COL))
    shell_power = spectra[1:3] / counts[None, :]
    shell_correlation = (spectra[0] / jnp.sqrt(spectra[1] * spectra[2] + 1e-06))[None]
    return (half_maps, shell_power, shell_correlation)


def solution(mesh):
    torus = Mesh(
        mesh.devices.reshape(mesh.shape["half"], 4, 4, mesh.shape["col"]),
        ("half", "row_0", "row_1", "col"),
    )
    in_specs = (P(HALF_ROW_COL, None, None, None), P(HALF_ROW_COL), P(HALF_ROW_COL, None), P())
    out_specs = (P("half", None, ROW, "col"), P(), P("half", None))
    return jax.shard_map(local, mesh=torus, in_specs=in_specs, out_specs=out_specs, check_vma=False)
```

profile of v0, /device:TPU:2, one launch (start us, length us, event | category | flops | bytes accessed | tf_op | source)
XLA Modules:
  0.0 170.0 jit_solution(13505677544732401227)
XLA Ops:
  0.6 57.2 %while.17 = (s32[]{:T(128)}, f32[3,64,4096]{2,1,0:T(8,128)}, s32[2,2]{1,0:T(2,128)}, bf16[2,2,64,4096]{3,2,1,0:T(8,128)(2,1)}, s32[2]{0:T(128)}, /*index=5*/bf16...) while((s32[]{:T(128)}, f32[3,64,4096]{2,1,0:T(8,128)}, ...), condition=%wide.region_1.2_spmd.clone, body=%wide.region_0.1_spmd.clone.sunk | while | flops 314609792 | bytes 29511420 | solution.py:103
  0.7 0.7 constant_dynamic-slice_fusion.2
  1.3 0.6 fusion.55
  1.9 2.9 %fusion.57 = (bf16[1,64,4096]{2,1,0:T(8,128)(2,1)S(1)}, bf16[1,64,4096]{2,1,0:T(8,128)(2,1)S(1)}) fusion(bf16[2,2,64,4096]{3,2,1,0:T(8,128)(2,1)} %get-tuple-element.314, s32[]{:T(128)} %get-tuple-element.300, s32[64]{0:T(128)S(1)} %get-tuple-element.281, s32[]{:T(128)} %bitcast.81, s32[]{:T(128)} %bitcast.82, s32[4096]{0:T(1024)S(1)} %get-tuple-element.284, ...), kind=kLoop, calls=%fused_computation.15.clone.1 | loop fusion | flops 2883584 | bytes 2130448 | tf_op jit(solution)/shard_map/convert.2
  4.8 1.6 convert_convert_fusion.2
  6.4 1.2 dynamic_slice.56
  9.6 2.4 %fusion.58 = bf16[3,64,4096]{2,1,0:T(8,128)(2,1)} fusion(bf16[1,64,4096]{2,1,0:T(8,128)(2,1)S(1)} %convert_convert_fusion.2, bf16[1,64,4096]{2,1,0:T(8,128)(2,1)S(1)} %get-tuple-element.287, bf16[1,64,4096]{2,1,0:T(8,128)(2,1)S(1)} %get-tuple-element.288, bf16[16,3,64,64]{3,2,1,0:T(8,128)(2,1)} %get-tuple-element.316, s32[]{:T(128)S(6)} %select_n.174), kind=kOutput, calls=%fused_computation.1.clone.1 | convolution fusion | flops 106168320 | bytes 3162116 | tf_op jit(solution)/shard_map/while/body/eval_jaxpr/ax,cxm->cam/dot_general | solution.py:47
  12.1 4.3 %reshape.637 = bf16[3,64,64,64]{3,2,1,0:T(8,128)(2,1)S(1)} reshape(bf16[3,64,4096]{2,1,0:T(8,128)(2,1)} %fusion.58) | data formatting | bytes 3145728 | tf_op jit(solution)/shard_map/while/body/eval_jaxpr/reshape | solution.py:50
  16.4 5.4 %fusion.59 = f32[3,64,64,64]{3,2,1,0:T(8,128)} fusion(bf16[3,64,64,64]{3,2,1,0:T(8,128)(2,1)S(1)} %reshape.637, bf16[16,3,64,64]{3,2,1,0:T(8,128)(2,1)} %get-tuple-element.316, s32[]{:T(128)S(6)} %select_n.174, s32[]{:T(128)S(6)} %add.406, s32[]{:T(128)S(6)} %add.404), kind=kOutput, calls=%fused_computation.2.clone.1 | convolution fusion | flops 202113024 | bytes 4753408 | tf_op jit(solution)/shard_map/while/body/eval_jaxpr/dz,cabz->cabd/dot_general | solution.py:54
  21.8 4.5 %reshape.638 = f32[3,64,4096]{2,1,0:T(8,128)S(1)} reshape(f32[3,64,64,64]{3,2,1,0:T(8,128)} %fusion.59) | data formatting | bytes 6291456 | tf_op jit(solution)/shard_map/while/body/eval_jaxpr/reshape | solution.py:57
  26.2 2.1 %select_add_fusion.2 = f32[3,64,4096]{2,1,0:T(8,128)} fusion(f32[3,64,4096]{2,1,0:T(8,128)S(1)} %reshape.638, f32[3,64,4096]{2,1,0:T(8,128)} %get-tuple-element.301, pred[]{:T(512)S(6)} %compare.17), kind=kLoop, calls=%fused_computation.4.clone.1 | loop fusion | flops 1572864 | bytes 9437185 | tf_op jit(solution)/shard_map/while/body/eval_jaxpr/add | solution.py:100
  28.3 0.7 constant_dynamic-slice_fusion.2
  29.6 2.9 %fusion.57 = (bf16[1,64,4096]{2,1,0:T(8,128)(2,1)S(1)}, bf16[1,64,4096]{2,1,0:T(8,128)(2,1)S(1)}) fusion(bf16[2,2,64,4096]{3,2,1,0:T(8,128)(2,1)} %get-tuple-element.314, s32[]{:T(128)} %get-tuple-element.300, s32[64]{0:T(128)S(1)} %get-tuple-element.281, s32[]{:T(128)} %bitcast.81, s32[]{:T(128)} %bitcast.82, s32[4096]{0:T(1024)S(1)} %get-tuple-element.284, ...), kind=kLoop, calls=%fused_computation.15.clone.1 | loop fusion | flops 2883584 | bytes 2130448 | tf_op jit(solution)/shard_map/convert.2
  32.5 1.6 convert_convert_fusion.2
  34.1 1.2 dynamic_slice.56
  37.3 2.4 %fusion.58 = bf16[3,64,4096]{2,1,0:T(8,128)(2,1)} fusion(bf16[1,64,4096]{2,1,0:T(8,128)(2,1)S(1)} %convert_convert_fusion.2, bf16[1,64,4096]{2,1,0:T(8,128)(2,1)S(1)} %get-tuple-element.287, bf16[1,64,4096]{2,1,0:T(8,128)(2,1)S(1)} %get-tuple-element.288, bf16[16,3,64,64]{3,2,1,0:T(8,128)(2,1)} %get-tuple-element.316, s32[]{:T(128)S(6)} %select_n.174), kind=kOutput, calls=%fused_computation.1.clone.1 | convolution fusion | flops 106168320 | bytes 3162116 | tf_op jit(solution)/shard_map/while/body/eval_jaxpr/ax,cxm->cam/dot_general | solution.py:47
  39.7 4.3 %reshape.637 = bf16[3,64,64,64]{3,2,1,0:T(8,128)(2,1)S(1)} reshape(bf16[3,64,4096]{2,1,0:T(8,128)(2,1)} %fusion.58) | data formatting | bytes 3145728 | tf_op jit(solution)/shard_map/while/body/eval_jaxpr/reshape | solution.py:50
  44.0 5.4 %fusion.59 = f32[3,64,64,64]{3,2,1,0:T(8,128)} fusion(bf16[3,64,64,64]{3,2,1,0:T(8,128)(2,1)S(1)} %reshape.637, bf16[16,3,64,64]{3,2,1,0:T(8,128)(2,1)} %get-tuple-element.316, s32[]{:T(128)S(6)} %select_n.174, s32[]{:T(128)S(6)} %add.406, s32[]{:T(128)S(6)} %add.404), kind=kOutput, calls=%fused_computation.2.clone.1 | convolution fusion | flops 202113024 | bytes 4753408 | tf_op jit(solution)/shard_map/while/body/eval_jaxpr/dz,cabz->cabd/dot_general | solution.py:54
  49.4 4.5 %reshape.638 = f32[3,64,4096]{2,1,0:T(8,128)S(1)} reshape(f32[3,64,64,64]{3,2,1,0:T(8,128)} %fusion.59) | data formatting | bytes 6291456 | tf_op jit(solution)/shard_map/while/body/eval_jaxpr/reshape | solution.py:57
  53.9 4.0 %select_add_fusion.2 = f32[3,64,4096]{2,1,0:T(8,128)} fusion(f32[3,64,4096]{2,1,0:T(8,128)S(1)} %reshape.638, f32[3,64,4096]{2,1,0:T(8,128)} %get-tuple-element.301, pred[]{:T(512)S(6)} %compare.17), kind=kLoop, calls=%fused_computation.4.clone.1 | loop fusion | flops 1572864 | bytes 9437185 | tf_op jit(solution)/shard_map/while/body/eval_jaxpr/add | solution.py:100
  57.8 3.1 %reshape.624 = f32[3,16,4,4096]{3,2,1,0:T(4,128)S(1)} reshape(f32[3,64,4096]{2,1,0:T(8,128)} %get-tuple-element.181) | data formatting | bytes 6291456 | tf_op jit(solution)/shard_map/reshape | solution.py:17
  60.9 1.9 %copy.13 = f32[16,3,4,4096]{3,2,1,0:T(4,128)} copy(f32[16,3,4,4096]{3,2,0,1:T(4,128)S(1)} %bitcast.84) | data formatting | bytes 6291456 | tf_op jit(solution)/shard_map/transpose | solution.py:17
  62.8 7.5 %all-to-all-start = ((f32[16,3,4,4096]{3,2,1,0:T(4,128)}), f32[16,3,4,4096]{3,2,1,0:T(4,128)S(1)}, u32[]{:S(2)}, u32[]{:S(2)}) async-start(f32[16,3,4,4096]{3,2,1,0:T(4,128)} %copy.13), calls=%async_computation | async-start | bytes 6291456 | tf_op jit(solution)/shard_map/all_to_all | solution.py:22
  70.3 41.1 %all-to-all-done = f32[16,3,4,4096]{3,2,1,0:T(4,128)S(1)} async-done(((f32[16,3,4,4096]{3,2,1,0:T(4,128)}), f32[16,3,4,4096]{3,2,1,0:T(4,128)S(1)}, u32[]{:S(2)}, u32[]{:S(2)}) %all-to-all-start) | async-done | bytes 3145760 | tf_op jit(solution)/shard_map/all_to_all | solution.py:22
  111.5 0.7 reduce_sum.36
  112.3 0.8 copy.14
  113.1 8.5 %all-to-all-start.1 = ((f32[8,3,4,512]{3,2,1,0:T(4,128)}), f32[8,3,4,512]{3,2,1,0:T(4,128)S(1)}, u32[]{:S(2)}, u32[]{:S(2)}) async-start(f32[8,3,4,512]{3,2,1,0:T(4,128)} %copy.14), calls=%async_computation.1 | async-start | bytes 393216 | tf_op jit(solution)/shard_map/all_to_all | solution.py:22
  121.8 9.6 %all-to-all-done.1 = f32[8,3,4,512]{3,2,1,0:T(4,128)S(1)} async-done(((f32[8,3,4,512]{3,2,1,0:T(4,128)}), f32[8,3,4,512]{3,2,1,0:T(4,128)S(1)}, u32[]{:S(2)}, u32[]{:S(2)}) %all-to-all-start.1) | async-done | bytes 196640 | tf_op jit(solution)/shard_map/all_to_all | solution.py:22
  131.7 1.0 collective-permute-done
  133.0 9.0 %all-reduce.2 = (f32[3,29]{1,0:T(4,128)S(1)}, f32[29]{0:T(128)S(1)}) all-reduce(f32[3,29]{1,0:T(4,128)S(1)} %fusion.23, f32[29]{0:T(128)S(1)} %convert_reduce_fusion), channel_id=1, replica_groups=mesh['half'=2,'row_0'=4,'row_1'=4,'col'=8] {'row_0'}, use_global_device_ids=true, to_apply=%region_5.6 | all-reduce | flops 116 | bytes 928 | tf_op jit(solution)/shard_map/psum | solution.py:33
  142.1 12.1 %all-reduce.1 = (f32[3,29]{1,0:T(4,128)S(1)}, f32[29]{0:T(128)S(1)}) all-reduce(f32[3,29]{1,0:T(4,128)S(1)} %get-tuple-element.219, f32[29]{0:T(128)S(1)} %get-tuple-element.220), channel_id=1, replica_groups=mesh['half'=2,'row_0'=4,'row_1'=4,'col'=8] {'row_1'}, use_global_device_ids=true, to_apply=%region_6.7 | all-reduce | flops 116 | bytes 928 | tf_op jit(solution)/shard_map/psum | solution.py:33
  154.2 14.7 %all-reduce = (f32[3,29]{1,0:T(4,128)S(1)}, f32[29]{0:T(128)S(1)}) all-reduce(f32[3,29]{1,0:T(4,128)S(1)} %get-tuple-element.217, f32[29]{0:T(128)S(1)} %get-tuple-element.218), channel_id=1, replica_groups=mesh['half'=2,'row_0'=4,'row_1'=4,'col'=8] {'col'}, use_global_device_ids=true, to_apply=%region_7.8 | all-reduce | flops 116 | bytes 928 | tf_op jit(solution)/shard_map/psum | solution.py:33
  (29 shorter events, 2.6 us)
Async XLA Ops:
  62.8 48.7 %all-to-all-start = ((f32[16,3,4,4096]{3,2,1,0:T(4,128)}), f32[16,3,4,4096]{3,2,1,0:T(4,128)S(1)}, u32[]{:S(2)}, u32[]{:S(2)}) async-start(f32[16,3,4,4096]{3,2,1,0:T(4,128)} %copy.13), calls=%async_computation | async-start | bytes 6291456 | tf_op jit(solution)/shard_map/all_to_all | solution.py:22
  113.1 18.2 %all-to-all-start.1 = ((f32[8,3,4,512]{3,2,1,0:T(4,128)}), f32[8,3,4,512]{3,2,1,0:T(4,128)S(1)}, u32[]{:S(2)}, u32[]{:S(2)}) async-start(f32[8,3,4,512]{3,2,1,0:T(4,128)} %copy.14), calls=%async_computation.1 | async-start | bytes 393216 | tf_op jit(solution)/shard_map/all_to_all | solution.py:22
  131.5 38.5 %copy-start = (f32[1,2,4,512]{3,2,1,0:T(4,128)}, f32[1,2,4,512]{3,2,1,0:T(4,128)S(1)}, u32[]{:S(2)}) copy-start(f32[1,2,4,512]{3,2,1,0:T(4,128)S(1)} %fusion.32) | copy-start | bytes 49156
  131.5 1.3 collective-permute-start
where the time goes:
time: 171 us; the launch traced here: 170 us
  waiting for transfers between devices  51.8 us (30%)
  blocking collectives  35.8 us (21%)
  local copies, waits for them, and re-layouts  28.5 us (17%)
  other arithmetic  17.3 us (10%)
  starting transfers between devices  16 us (9%)
  matrix products  15.9 us (9%)
  loops' own time  3.98 us (2%)
    all_to_all x2, waiting for transfers between devices, summed_on_arrival(): parts = lax.all_to_all(split_up(x, dim, size), axis, 0, 0, tiled=True)  50.8 us
    psum x3, blocking collectives, one_axis_at_a_time(): return functools.reduce(lax.psum, axes, x)  35.8 us
    all_to_all x2, starting transfers between devices, summed_on_arrival(): parts = lax.all_to_all(split_up(x, dim, size), axis, 0, 0, tiled=True)  15.9 us
    dot_general x2, matrix products, interpolate(): jnp.einsum('dz,cabz->cabd', kernels[2], along_second, preferred_element_t...  10.8 us
    another operation x4, other arithmetic  8.98 us
    reshape x2, local copies, waits for them, and re-layouts, interpolate(): return along_third.reshape(components, grid_size, grid_size * grid_size)  8.9 us
    reshape x2, local copies, waits for them, and re-layouts, interpolate(): along_first.reshape(components, grid_size, grid_size, grid_size)  8.61 us
    add x2, other arithmetic, insert_one(): return partial_value + interpolate(stacked, kernels, grid_size)  6.01 us
  transfers between devices with their start and end apart: 3, of which 3 were waited for; matrix products, arithmetic and copies ran while one was open for 0% of the time, Pallas kernels for 0%

commit v1 on v0

v1 whole, which is shorter than its diff:
```python
import functools

import jax
import jax.numpy as jnp
from jax import lax
from jax.experimental import pallas as pl
from jax.experimental.pallas import tpu as pltpu
from jax.sharding import Mesh
from jax.sharding import PartitionSpec as P

SHELLS = 29
GRID = 64
BINS = 16
STRIDE = 72
HALF_ROW_COL = ("half", "row_0", "row_1", "col")
MESH = pl.DeviceIdType.MESH
F32 = jnp.float32
BF16 = jnp.bfloat16


def iota(shape, dim):
    return lax.broadcasted_iota(jnp.int32, shape, dim)


def insert_kernel(bin_ref, slope_ref, particle_ref, table_ref, v0_ref, v1_ref, info_ref, mid0_ref, mid1_ref):
    lane = iota((1, 128), 1)
    row = jnp.zeros((1, 128), jnp.int32)
    for particle in range(2):
        row = jnp.where(lane == particle, bin_ref[particle], row)
        for side in range(2):
            row = jnp.where(lane == 2 + 2 * particle + side, slope_ref[particle, side], row)
    info_ref[...] = row

    wave_first = iota((GRID, 128), 0) - 32
    wave_third = (iota((GRID, 128), 1) & 63) - 32
    same_side = wave_first * wave_third >= 0
    block_row = iota((256, 256), 0) // 64
    block_col = iota((256, 256), 1) // 64
    matching = (block_row // 2 == block_col % 2) & (block_row % 2 == block_col // 2)

    for particle, mid_ref in enumerate((mid0_ref, mid1_ref)):
        limit = jnp.where(same_side, slope_ref[particle, 0], slope_ref[particle, 1])
        inside = 16 * jnp.abs(wave_third) <= limit * jnp.abs(wave_first)
        weight = inside.astype(F32).astype(BF16)
        which = bin_ref[particle]
        along_first = table_ref[which, 0]
        third = jnp.transpose(table_ref[which, 2].astype(F32))
        third = jnp.concatenate([third, third], axis=1)
        third = jnp.concatenate([third, third], axis=1)
        third = jnp.concatenate([third, third, third, third], axis=0)
        along_third = jnp.where(matching, third, 0.0).astype(BF16)

        def pairs(step, carry):
            for inner in range(4):
                pair = step * 4 + inner
                columns = pl.ds(pl.multiple_of(pair * 128, 128), 128)
                data = jnp.concatenate(
                    [particle_ref[particle, part, :, columns] * weight for part in range(2)], axis=1
                )
                first = jnp.dot(along_first, data, preferred_element_type=F32).astype(BF16)
                both = jnp.dot(first, along_third, preferred_element_type=F32)
                start = pl.multiple_of(pair * (2 * STRIDE), 8)
                mid_ref[pl.ds(start, GRID), :] = both[:, :128]
                mid_ref[pl.ds(start + STRIDE, GRID), :] = both[:, 128:]
            return carry

        lax.fori_loop(0, 8, pairs, 0)

    along_second = jnp.concatenate(
        [table_ref[bin_ref[particle], 1].astype(F32) for particle in range(2)], axis=1
    ).astype(BF16)

    for slow in range(4):

        def slabs(fast, carry):
            for color, out_ref in enumerate((v0_ref, v1_ref)):
                places = []
                for inner in range(2):
                    first = 16 * slow + 4 * fast + 2 * color + inner
                    if color == 1:
                        first = 16 * fast + 4 * slow + 2 * color + inner
                    rows = [
                        mid_ref[pl.ds(first, GRID, stride=STRIDE), :]
                        for mid_ref in (mid0_ref, mid1_ref)
                    ]
                    places.append(jnp.concatenate(rows, axis=0).astype(BF16))
                slab = jnp.dot(
                    along_second, jnp.concatenate(places, axis=1), preferred_element_type=F32
                )
                out_ref[slow, fast, 0] = slab[:, :128]
                out_ref[slow, fast, 1] = slab[:, 128:]
            return carry

        lax.fori_loop(0, 4, slabs, 0)


def insert(particles, orient_bin, tilt_slope, interp_table):
    smem = pl.BlockSpec(memory_space=pltpu.SMEM)
    vmem = pl.BlockSpec(memory_space=pltpu.VMEM)
    volume = jax.ShapeDtypeStruct((4, 4, 2, GRID, 128), F32)
    return pl.pallas_call(
        insert_kernel,
        out_shape=(volume, volume, jax.ShapeDtypeStruct((1, 128), jnp.int32)),
        in_specs=[smem, smem, vmem, vmem],
        out_specs=(vmem, vmem, vmem),
        scratch_shapes=[pltpu.VMEM((GRID * STRIDE, 128), F32)] * 2,
        compiler_params=pltpu.CompilerParams(vmem_limit_bytes=32 * 2**20),
        name="insert",
    )(orient_bin, tilt_slope, particles, interp_table)


def weight_sums(info, row, col, table_ref, count_ref, first_ref, second_ref):
    lane = iota((128, 128), 1)
    side_lane = lane & 63
    bins, slopes = [], []
    for particle in range(2):
        bins.append((info[:, particle : particle + 1] == lane).astype(F32))
        limit = jnp.where(
            lane < 64, info[:, 2 + 2 * particle : 3 + 2 * particle], info[:, 3 + 2 * particle : 4 + 2 * particle]
        )
        slopes.append((limit == side_lane).astype(F32))
    bins = jnp.concatenate([jnp.transpose(part)[:BINS] for part in bins], axis=1).astype(BF16)
    slopes = jnp.concatenate(slopes, axis=0).astype(BF16)
    histogram = jnp.dot(bins, slopes, preferred_element_type=F32).astype(BF16)

    wave_third = (iota((128, 128), 1) & 63) - 32
    reach = (16 * jnp.abs(wave_third)).astype(F32)
    limit = (iota((128, 128), 0) & 63).astype(F32)
    same_side = iota((128, 128), 0) < 64
    nonneg_third, nonpos_third = wave_third >= 0, wave_third <= 0

    def planes(first, carry):
        wave_first = first - 32
        agree = (
            ((wave_first > 0) & nonneg_third) | ((wave_first < 0) & nonpos_third) | (wave_first == 0)
        )
        inside = (reach <= limit * jnp.abs(wave_first).astype(F32)) & (agree == same_side)
        counts = jnp.dot(histogram, inside.astype(F32).astype(BF16), preferred_element_type=F32)
        count_ref[pl.ds(pl.multiple_of(first * BINS, BINS), BINS), :] = counts
        return carry

    lax.fori_loop(0, GRID, planes, 0)

    bin_lane = iota((GRID, 128), 1)
    second = jnp.zeros((GRID, 128), F32)
    for which in range(BINS):
        counts = count_ref[pl.ds(which, GRID, stride=BINS), :].astype(BF16)
        first_ref[which] = jnp.dot(table_ref[which, 0], counts, preferred_element_type=F32)
        total = jnp.sum(table_ref[which, 1].astype(F32), axis=1, keepdims=True)
        second = jnp.where(bin_lane == which, total, second)
    second_ref[...] = second
    second = second_ref[pl.ds(pl.multiple_of(col * 8, 8), 8), :]
    sums = [jnp.zeros((8, 128), F32) for _ in range(4)]
    for which in range(BINS):
        first = first_ref[which, pl.ds(row * 4, 4), :][:, :GRID]
        high = first.astype(BF16)
        low = (first - high.astype(F32)).astype(BF16)
        third = jnp.concatenate([table_ref[which, 2]] * 2, axis=0)
        contract = functools.partial(
            lax.dot_general, dimension_numbers=(((1,), (1,)), ((), ())), preferred_element_type=F32
        )
        plane = contract(high, third) + contract(low, third)
        for index in range(4):
            sums[index] = sums[index] + second[:, which : which + 1] * plane[index : index + 1]
    return sums


class Ring4:
    def __init__(self, axis, source, buffer, send, recv):
        self.axis, self.source, self.buffer, self.send, self.recv = axis, source, buffer, send, recv
        self.me = lax.axis_index(axis)
        self.right, self.far, self.left = ((self.me + step) % 4 for step in (1, 2, 3))
        self.copies = [None] * 6

    def copy(self, slot, source, target):
        self.copies[slot] = pltpu.make_async_remote_copy(
            src_ref=source,
            dst_ref=self.buffer.at[slot],
            send_sem=self.send.at[slot],
            recv_sem=self.recv.at[slot],
            device_id={self.axis: target},
            device_id_type=MESH,
        )
        self.copies[slot].start()

    def begin(self):
        self.copy(0, self.source(self.far, 0), self.right)
        self.copy(3, self.source(self.far, 1), self.left)
        self.copy(2, self.source(self.right, 1), self.right)
        self.copy(5, self.source(self.left, 0), self.left)

    def forward(self):
        self.copies[0].wait_recv()
        self.buffer[0] = self.buffer[0] + self.source(self.right, 0)[...]
        self.copy(1, self.buffer.at[0], self.right)
        self.copies[3].wait_recv()
        self.buffer[3] = self.buffer[3] + self.source(self.left, 1)[...]
        self.copy(4, self.buffer.at[3], self.left)

    def finish(self, result):
        for half, near, other in ((0, 1, 5), (1, 4, 2)):
            self.copies[other].wait_recv()
            self.copies[near].wait_recv()
            result(half)[...] = self.source(self.me, half)[...] + self.buffer[near] + self.buffer[other]

    def drain(self):
        for copy in self.copies:
            copy.wait_send()


def exchange(axis, size, source, target, send, recv):
    me = lax.axis_index(axis)
    copies = []
    for step in range(1, size):
        peer = (me + step) % size
        copy = pltpu.make_async_remote_copy(
            src_ref=source(peer),
            dst_ref=target,
            send_sem=send.at[step],
            recv_sem=recv.at[step],
            device_id={axis: peer},
            device_id_type=MESH,
        )
        copy.start()
        copies.append(copy)
    return copies


def shell_rows(sums_first, sums_second, row, col):
    wave_second = iota((8, 128), 0) + col * 8 - 32
    wave_third = (iota((8, 128), 1) & 63) - 32
    plane = wave_second * wave_second + wave_third * wave_third
    radius = []
    for index in range(4):
        wave_first = row * 4 + index - 32
        radius.append(plane + wave_first * wave_first)
    real = iota((8, 128), 1) < 64
    values = [
        [first * second for first, second in zip(sums_first, sums_second)],
        [first * first for first in sums_first],
        [second * second for second in sums_second],
        [jnp.where(real, 1.0, 0.0).astype(F32)] * 4,
    ]
    rows = [[] for _ in range(4)]
    for shell in range(32):
        low = 0 if shell == 0 else (shell + 3) ** 2
        high = (shell + 4) ** 2 if shell < SHELLS else low
        masks = [(r >= low) & (r < high) for r in radius]
        for kind in range(4):
            parts = [jnp.where(m, v, 0.0) for m, v in zip(masks, values[kind])]
            total = (parts[0] + parts[1]) + (parts[2] + parts[3])
            rows[kind].append(jnp.sum(total, axis=0, keepdims=True))
    stacked = jnp.concatenate([row for kind in rows for row in kind], axis=0)
    ones = jnp.ones((8, 128), F32)
    return lax.dot_general(
        ones,
        stacked,
        dimension_numbers=(((1,), (1,)), ((), ())),
        precision=lax.Precision.HIGHEST,
        preferred_element_type=F32,
    )[:1]


def reduce_kernel(
    info_ref, table_ref, v0_ref, v1_ref, map_ref, stat_ref,
    ring_a, ring_b, ring_c, ring_d, part0, part1, slab, planes, gathered, own, other, stat_x, stat_y, stat_z,
    count_ref, first_ref, second_ref, ring_send, ring_recv, small_send, small_recv,
):
    half, x, y, z = (lax.axis_index(name) for name in HALF_ROW_COL)
    row = x * 4 + y
    barrier = pltpu.get_barrier_semaphore()
    for axis, size in (("row_0", 4), ("row_1", 4), ("col", 8), ("half", 2)):
        for step in range(1, size):
            peer = (lax.axis_index(axis) + step) % size
            pl.semaphore_signal(barrier, inc=1, device_id={axis: peer}, device_id_type=MESH)
    pl.semaphore_wait(barrier, 14)

    def small(index):
        return small_send.at[index], small_recv.at[index]

    def outer(ref):
        return lambda owner, side: ref.at[owner, pl.ds(2 * side, 2)]

    pending = []
    gathered[z, y, x] = info_ref[...]
    spread = exchange("row_0", 4, lambda peer: info_ref, gathered.at[z, y, x], *small(0))
    pending += spread
    first = [
        Ring4("row_0", outer(v0_ref), ring_a, ring_send.at[0], ring_recv.at[0]),
        Ring4("row_1", outer(v1_ref), ring_b, ring_send.at[1], ring_recv.at[1]),
    ]
    for ring in first:
        ring.begin()
    for copy in spread:
        copy.wait_recv()
    spread = exchange("row_1", 4, lambda peer: gathered.at[z, y], gathered.at[z, y], *small(1))
    pending += spread
    for ring in first:
        ring.forward()
    for copy in spread:
        copy.wait_recv()
    spread = exchange("col", 8, lambda peer: gathered.at[z], gathered.at[z], *small(2))
    pending += spread
    for ring, part in zip(first, (part0, part1)):
        ring.finish(lambda side, part=part: part.at[pl.ds(2 * side, 2)])

    second = [
        Ring4("row_1", lambda owner, side: part0.at[owner, side], ring_c, ring_send.at[2], ring_recv.at[2]),
        Ring4("row_0", lambda owner, side: part1.at[owner, side], ring_d, ring_send.at[3], ring_recv.at[3]),
    ]
    for ring in second:
        ring.begin()
    for copy in spread:
        copy.wait_recv()
    for ring in second:
        ring.forward()
    for color, ring in enumerate(second):
        ring.finish(lambda side, color=color: slab.at[2 * color + side])

    spread = exchange(
        "col", 8, lambda peer: slab.at[:, pl.ds(pl.multiple_of(peer * 8, 8), 8)], planes.at[z], *small(3)
    )
    pending += spread
    weights = weight_sums(
        gathered[...].reshape(128, 128), row, z, table_ref, count_ref, first_ref, second_ref
    )
    for copy in spread:
        copy.wait_recv()
    for index in range(4):
        total = slab[index, pl.ds(pl.multiple_of(z * 8, 8), 8)]
        for step in range(1, 8):
            total = total + planes[(z + step) % 8, index]
        own[index] = total / (weights[index] + 1.0)
    partner = exchange("half", 2, lambda peer: own, other, *small(4))
    pending += partner
    map_ref[...] = own[...]
    partner[0].wait_recv()
    on_first = half == 0
    mine = [own[index] for index in range(4)]
    theirs = [other[index] for index in range(4)]
    maps_first = [jnp.where(on_first, a, b) for a, b in zip(mine, theirs)]
    maps_second = [jnp.where(on_first, b, a) for a, b in zip(mine, theirs)]
    stat = shell_rows(maps_first, maps_second, row, z)
    for number, (axis, size, ref) in enumerate((("row_0", 4, stat_x), ("row_1", 4, stat_y), ("col", 8, stat_z))):
        me = lax.axis_index(axis)
        ref[me] = stat
        spread = exchange(axis, size, lambda peer: ref.at[me], ref.at[me], *small(5 + number))
        pending += spread
        for copy in spread:
            copy.wait_recv()
        stat = ref[0]
        for index in range(1, size):
            stat = stat + ref[index]
    stat_ref[...] = stat
    for ring in first + second:
        ring.drain()
    for copy in pending:
        copy.wait_send()


def reduce_maps(info, interp_table, v0, v1):
    vmem = pl.BlockSpec(memory_space=pltpu.VMEM)
    big, little = pltpu.VMEM((6, 2, 2, GRID, 128), F32), pltpu.VMEM((6, GRID, 128), F32)
    stat = lambda size: pltpu.VMEM((size, 1, 128), F32)
    return pl.pallas_call(
        reduce_kernel,
        out_shape=(jax.ShapeDtypeStruct((4, 8, 128), F32), jax.ShapeDtypeStruct((1, 128), F32)),
        in_specs=[vmem] * 4,
        out_specs=(vmem, vmem),
        scratch_shapes=[
            big,
            big,
            little,
            little,
            pltpu.VMEM((4, 2, GRID, 128), F32),
            pltpu.VMEM((4, 2, GRID, 128), F32),
            pltpu.VMEM((4, GRID, 128), F32),
            pltpu.VMEM((8, 4, 8, 128), F32),
            pltpu.VMEM((8, 4, 4, 1, 128), jnp.int32),
            pltpu.VMEM((4, 8, 128), F32),
            pltpu.VMEM((4, 8, 128), F32),
            stat(4),
            stat(4),
            stat(8),
            pltpu.VMEM((GRID * BINS, 128), F32),
            pltpu.VMEM((BINS, GRID, 128), F32),
            pltpu.VMEM((GRID, 128), F32),
            pltpu.SemaphoreType.DMA((4, 6)),
            pltpu.SemaphoreType.DMA((4, 6)),
            pltpu.SemaphoreType.DMA((8, 8)),
            pltpu.SemaphoreType.DMA((8, 8)),
        ],
        compiler_params=pltpu.CompilerParams(
            collective_id=0, has_side_effects=True, vmem_limit_bytes=32 * 2**20
        ),
        name="reduce",
    )(info, interp_table, v0, v1)


def local(particles, orient_bin, tilt_slope, interp_table):
    v0, v1, info = insert(particles, orient_bin, tilt_slope, interp_table)
    maps, stat = reduce_maps(info, interp_table, v0, v1)
    half_maps = maps.reshape(4, 8, 2, GRID).transpose(2, 0, 1, 3).reshape(1, 2, 4, 8 * GRID)
    cross, power_first, power_second, counts = (
        stat[0, 32 * kind : 32 * kind + SHELLS] for kind in range(4)
    )
    shell_power = jnp.stack([power_first, power_second]) / counts[None, :]
    shell_correlation = (cross / jnp.sqrt(power_first * power_second + 1e-06))[None]
    return half_maps, shell_power, shell_correlation


def solution(mesh):
    torus = Mesh(
        mesh.devices.reshape(mesh.shape["half"], 4, 4, mesh.shape["col"]), HALF_ROW_COL
    )
    in_specs = (P(HALF_ROW_COL, None, None, None), P(HALF_ROW_COL), P(HALF_ROW_COL, None), P())
    out_specs = (P("half", None, ("row_0", "row_1"), "col"), P(), P("half", None))
    return jax.shard_map(local, mesh=torus, in_specs=in_specs, out_specs=out_specs, check_vma=False)
```

time: 171 us -> 69.2 us (0.40)
  the two profiles are of different devices: /device:TPU:2 before, /device:TPU:1 now
where the time goes in v1:
time: 69.2 us; the launch traced here: 69 us
  Pallas kernels  62.3 us (90%)
  local copies, waits for them, and re-layouts  4.83 us (7%)
  other arithmetic  1.16 us (2%)
    pallas_call x1, Pallas kernels, reduce_maps(): pl.pallas_call(reduce_kernel, out_shape=(jax.ShapeDtypeStruct((4, 8, 128)...  51.8 us
    pallas_call x1, Pallas kernels, insert(): pl.pallas_call(insert_kernel, out_shape=(volume, volume, jax.ShapeDtypeSt...  10.5 us
    unnamed x10, local copies, waits for them, and re-layouts  4.05 us

profile of v1, /device:TPU:1, one launch (start us, length us, event | category | flops | bytes accessed | tf_op | source)
XLA Modules:
  0.0 69.0 jit_solution(5846240566792748303)
XLA Ops:
  0.6 0.0 copy-start
  0.6 1.1 %copy-done = bf16[16,3,64,64]{3,2,1,0:T(8,128)(2,1)S(1)} copy-done((bf16[16,3,64,64]{3,2,1,0:T(8,128)(2,1)S(1)}, bf16[16,3,64,64]{3,2,1,0:T(8,128)(2,1)}, u32[]{:S(2)}) %copy-start) | copy-done | bytes 393240
  1.8 0.0 copy-start.2
  1.8 1.6 %copy-done.2 = bf16[2,2,64,4096]{3,2,1,0:T(8,128)(2,1)S(1)} copy-done((bf16[2,2,64,4096]{3,2,1,0:T(8,128)(2,1)S(1)}, bf16[2,2,64,4096]{3,2,1,0:T(8,128)(2,1)}, u32[]{:S(2)}) %copy-start.2) | copy-done | bytes 2097176
  3.4 0.0 copy-start.3
  3.4 0.7 copy-done.3
  4.0 0.0 copy-start.4
  4.0 0.7 copy-done.4
  4.7 0.0 copy-start.1
  4.7 10.5 %insert.1 = (f32[4,4,2,64,128]{4,3,2,1,0:T(8,128)S(1)}, f32[4,4,2,64,128]{4,3,2,1,0:T(8,128)S(1)}, s32[1,128]{1,0:T(1,128)S(1)}) custom-call(s32[2]{0:T(128)S(1)} %copy-done.4, s32[2,2]{1,0:T(2,128)S(1)} %copy-done.3, bf16[2,2,64,4096]{3,2,1,0:T(8,128)(2,1)S(1)} %copy-done.2, bf16[16,3,64,64]{3,2,1,0:T(8,128)(2,1)S(1)} %copy-done), custom_call_target="tpu_custom_call" | custom-call | tf_op jit(solution)/shard_map/insert/pallas_call | solution.py:101
  15.2 0.0 copy-done.1
  15.2 51.8 %reduce.1 = (f32[4,8,128]{2,1,0:T(8,128)S(1)}, f32[1,128]{1,0:T(1,128)S(1)}) custom-call(s32[1,128]{1,0:T(1,128)S(1)} %get-tuple-element.8.info_ref, bf16[16,3,64,64]{3,2,1,0:T(8,128)(2,1)S(1)} %copy-done.1, f32[4,4,2,64,128]{4,3,2,1,0:T(8,128)S(1)} %get-tuple-element.9.v0_ref, f32[4,4,2,64,128]{4,3,2,1,0:T(8,128)S(1)} %get-tuple-element.10.v1_ref), custom_call_target="tpu_custom_call" | custom-call | tf_op jit(solution)/shard_map/reduce/pallas_call | solution.py:365
  67.0 0.6 rsqrt_multiply_fusion
  67.6 0.6 maximum_divide_fusion
  68.2 0.1 reshape.12
  68.3 0.7 reshape.13
  (1 shorter events, 0.0 us)
Async XLA Ops:
  0.6 1.1 %copy-start = (bf16[16,3,64,64]{3,2,1,0:T(8,128)(2,1)S(1)}, bf16[16,3,64,64]{3,2,1,0:T(8,128)(2,1)}, u32[]{:S(2)}) copy-start(bf16[16,3,64,64]{3,2,1,0:T(8,128)(2,1)} %table_ref.3) | copy-start | bytes 1179652
  1.8 1.6 %copy-start.2 = (bf16[2,2,64,4096]{3,2,1,0:T(8,128)(2,1)S(1)}, bf16[2,2,64,4096]{3,2,1,0:T(8,128)(2,1)}, u32[]{:S(2)}) copy-start(bf16[2,2,64,4096]{3,2,1,0:T(8,128)(2,1)} %particle_ref.1) | copy-start | bytes 6291460
  3.4 0.7 copy-start.3
  4.0 0.7 copy-start.4
  4.7 10.5 %copy-start.1 = (bf16[16,3,64,64]{3,2,1,0:T(8,128)(2,1)S(1)}, bf16[16,3,64,64]{3,2,1,0:T(8,128)(2,1)}, u32[]{:S(2)}) copy-start(bf16[16,3,64,64]{3,2,1,0:T(8,128)(2,1)} %table_ref.3) | copy-start | bytes 1179652

commit v2 on v0

v2 whole, which is shorter than its diff:
```python
import functools

import jax
import jax.numpy as jnp
from jax import lax
from jax.experimental import pallas as pl
from jax.experimental.pallas import tpu as pltpu
from jax.sharding import Mesh
from jax.sharding import PartitionSpec as P

SHELLS = 29
GRID = 64
BINS = 16
STRIDE = 24
HALF_ROW_COL = ("half", "row_0", "row_1", "col")
MESH = pl.DeviceIdType.MESH
F32 = jnp.float32
BF16 = jnp.bfloat16


def iota(shape, dim):
    return lax.broadcasted_iota(jnp.int32, shape, dim)


def owner_rows(x, y):
    index = iota((GRID, GRID), 0)
    group, color, other, inner = index // 16, (index // 8) % 2, (index // 2) % 4, index % 2
    shift = jnp.where(group == 0, 2, jnp.where(group == 1, 1, jnp.where(group == 2, 3, 0)))
    main = (jnp.where(color == 0, x, y) + shift) % 4
    plane = jnp.where(color == 0, 16 * main + 4 * other, 16 * other + 4 * main + 2) + inner
    return (plane == iota((GRID, GRID), 1)).astype(F32).astype(BF16)


def along_first(particle, order, bins, slopes, data, table, first):
    wave_first = iota((GRID, 128), 0) - 32
    wave_third = (iota((GRID, 128), 1) & 63) - 32
    limit = jnp.where(wave_first * wave_third >= 0, slopes[particle, 0], slopes[particle, 1])
    inside = 16 * jnp.abs(wave_third) <= limit * jnp.abs(wave_first)
    weight = inside.astype(F32).astype(BF16)
    kernel = jnp.dot(order, table[bins[particle], 0], preferred_element_type=F32).astype(BF16)

    def pairs(step, carry):
        for inner in range(16):
            pair = step * 16 + inner
            columns = pl.ds(pl.multiple_of(pair * 128, 128), 128)
            both = jnp.concatenate([data[particle, part, :, columns] * weight for part in range(2)], axis=1)
            first[particle, pair] = jnp.dot(kernel, both, preferred_element_type=F32).astype(BF16)
        return carry

    lax.fori_loop(0, 2, pairs, 0)


def third_operator(kernel):
    block_row = iota((256, 256), 0) // 64
    block_col = iota((256, 256), 1) // 64
    matching = (block_row // 2 == block_col % 2) & (block_row % 2 == block_col // 2)
    third = jnp.transpose(kernel.astype(F32))
    third = jnp.concatenate([third, third], axis=1)
    third = jnp.concatenate([third, third], axis=1)
    third = jnp.concatenate([third, third, third, third], axis=0)
    return jnp.where(matching, third, 0.0).astype(BF16)


def insert_group(group, operators, second, first, middles, volume):
    rows = pl.ds(16 * group, 16)
    for particle, middle in enumerate(middles):
        lines = first[particle, :, rows, :].reshape(512, 256)
        lines = jnp.dot(lines, operators[particle], preferred_element_type=F32)
        for pair in range(32):
            middle[pl.ds(2 * pair * STRIDE, 16), :] = lines[16 * pair : 16 * pair + 16, :128]
            middle[pl.ds((2 * pair + 1) * STRIDE, 16), :] = lines[16 * pair : 16 * pair + 16, 128:]
    for place in range(8):
        planes = []
        for inner in range(2):
            sides = [middle[pl.ds(2 * place + inner, GRID, stride=STRIDE), :] for middle in middles]
            planes.append(jnp.concatenate(sides, axis=0).astype(BF16))
        slab = jnp.dot(second, jnp.concatenate(planes, axis=1), preferred_element_type=F32)
        for inner in range(2):
            volume[group, place // 4, inner, place % 4] = slab[:, 128 * inner : 128 * inner + 128]


def bin_counts(infos, count_ref):
    lane = iota((128, 128), 1)
    histograms = []
    for info in infos:
        bins, slopes = [], []
        for particle in range(2):
            bins.append((info[:, particle : particle + 1] == lane).astype(F32))
            limit = jnp.where(
                lane < 64,
                info[:, 2 + 2 * particle : 3 + 2 * particle],
                info[:, 3 + 2 * particle : 4 + 2 * particle],
            )
            slopes.append((limit == (lane & 63)).astype(F32))
        bins = jnp.concatenate([jnp.transpose(part)[:BINS] for part in bins], axis=1).astype(BF16)
        slopes = jnp.concatenate(slopes, axis=0).astype(BF16)
        histograms.append(jnp.dot(bins, slopes, preferred_element_type=F32))
    histogram = jnp.concatenate(histograms, axis=0).astype(BF16)

    wave_third = (iota((128, 128), 1) & 63) - 32
    reach = (16 * jnp.abs(wave_third)).astype(F32)
    limit = (iota((128, 128), 0) & 63).astype(F32)
    same_side = iota((128, 128), 0) < 64
    nonneg_third, nonpos_third = wave_third >= 0, wave_third <= 0

    def planes(step, carry):
        for inner in range(4):
            first = step * 4 + inner
            wave_first = first - 32
            agree = (
                ((wave_first > 0) & nonneg_third) | ((wave_first < 0) & nonpos_third) | (wave_first == 0)
            )
            inside = (reach <= limit * jnp.abs(wave_first).astype(F32)) & (agree == same_side)
            counts = jnp.dot(histogram, inside.astype(F32).astype(BF16), preferred_element_type=F32)
            count_ref[pl.ds(pl.multiple_of(first * 2 * BINS, 2 * BINS), 2 * BINS), :] = counts
        return carry

    lax.fori_loop(0, GRID // 4, planes, 0)


def insert_counts(table, count_ref, first_ref, second_ref):
    bin_lane = iota((GRID, 128), 1)
    second = jnp.zeros((GRID, 128), F32)
    for which in range(BINS):
        counts = [count_ref[pl.ds(BINS * half + which, GRID, stride=2 * BINS), :] for half in range(2)]
        counts = jnp.concatenate(counts, axis=1).astype(BF16)
        lines = jnp.dot(table[which, 0], counts, preferred_element_type=F32)
        for half in range(2):
            first_ref[half, which] = lines[:, 128 * half : 128 * half + 128]
        total = jnp.sum(table[which, 1].astype(F32), axis=1, keepdims=True)
        second = jnp.where(bin_lane == which, total, second)
    second_ref[...] = second


def weight_sums(plane, col, table, first_ref, second_ref, weight_ref):
    second = second_ref[pl.ds(pl.multiple_of(col * 8, 8), 8), :]
    contract = functools.partial(
        lax.dot_general, dimension_numbers=(((1,), (1,)), ((), ())), preferred_element_type=F32
    )
    sums = [jnp.zeros((8, 128), F32) for _ in range(4)]
    for which in range(BINS):
        first = jnp.concatenate([first_ref[half, which, pl.ds(plane, 2), :] for half in range(2)], axis=0)[:, :GRID]
        high = first.astype(BF16)
        low = (first - high.astype(F32)).astype(BF16)
        third = jnp.concatenate([table[which, 2]] * 2, axis=0)
        lines = contract(high, third) + contract(low, third)
        for index in range(4):
            sums[index] = sums[index] + second[:, which : which + 1] * lines[index : index + 1]
    for index in range(4):
        weight_ref[index // 2, index % 2] = sums[index]


def remote(source, target, send, recv, device):
    copy = pltpu.make_async_remote_copy(
        src_ref=source, dst_ref=target, send_sem=send, recv_sem=recv, device_id=device, device_id_type=MESH
    )
    copy.start()
    return copy


class Ring4:
    def __init__(self, axis, source, buffer, send, recv):
        self.axis, self.source, self.buffer, self.send, self.recv = axis, source, buffer, send, recv
        me = lax.axis_index(axis)
        self.right, self.left = (me + 1) % 4, (me + 3) % 4
        self.copies = [None] * 6

    def copy(self, slot, source, target):
        self.copies[slot] = remote(
            source, self.buffer.at[slot], self.send.at[slot], self.recv.at[slot], {self.axis: target}
        )

    def send_far(self):
        self.copy(0, self.source(0, 0), self.right)
        self.copy(3, self.source(0, 1), self.left)

    def send_right(self):
        self.copy(2, self.source(1, 1), self.right)

    def send_left(self):
        self.copy(5, self.source(2, 0), self.left)

    def forward(self):
        self.copies[0].wait_recv()
        self.buffer[0] = self.buffer[0] + self.source(1, 0)[...]
        self.copy(1, self.buffer.at[0], self.right)
        self.copies[3].wait_recv()
        self.buffer[3] = self.buffer[3] + self.source(2, 1)[...]
        self.copy(4, self.buffer.at[3], self.left)

    def finish(self, result):
        for half, near, other in ((0, 1, 5), (1, 4, 2)):
            self.copies[other].wait_recv()
            self.copies[near].wait_recv()
            result[pl.ds(2 * half, 2)] = (
                self.source(3, half)[...] + self.buffer[near] + self.buffer[other]
            )


def exchange(me, size, place, source, target, send, recv):
    copies = []
    for step in range(1, size):
        peer = (me + step) % size
        copies.append(remote(source(peer), target, send.at[step], recv.at[step], place(peer)))
    return copies


def arrived(copies):
    for copy in copies:
        copy.wait_recv()


def shell_rows(sums_first, sums_second, plane, col):
    wave_second = iota((8, 128), 0) + col * 8 - 32
    wave_third = (iota((8, 128), 1) & 63) - 32
    rest = wave_second * wave_second + wave_third * wave_third
    radius = []
    for index in range(2):
        wave_first = plane + index - 32
        radius.append(rest + wave_first * wave_first)
    real = iota((8, 128), 1) < 64
    values = [
        [first * second for first, second in zip(sums_first, sums_second)],
        [first * first for first in sums_first],
        [second * second for second in sums_second],
        [jnp.where(real, 1.0, 0.0).astype(F32)] * 2,
    ]
    rows = [[] for _ in range(4)]
    for shell in range(32):
        low = 0 if shell == 0 else (shell + 3) ** 2
        high = (shell + 4) ** 2 if shell < SHELLS else low
        masks = [(r >= low) & (r < high) for r in radius]
        for kind in range(4):
            parts = [jnp.where(m, v, 0.0) for m, v in zip(masks, values[kind])]
            rows[kind].append(jnp.sum(parts[0] + parts[1], axis=0, keepdims=True))
    stacked = jnp.concatenate([row for kind in rows for row in kind], axis=0)
    return lax.dot_general(
        jnp.ones((8, 128), F32),
        stacked,
        dimension_numbers=(((1,), (1,)), ((), ())),
        precision=lax.Precision.HIGHEST,
        preferred_element_type=F32,
    )[:1]


def kernel(
    particle_hbm, bin_hbm, slope_hbm, table_hbm, map_ref, power_ref, correlation_ref,
    data, bins, slopes, table, first, middle0, middle1, volume,
    ring_buffer, part, spread_buffer, slab, planes, info_ref, gathered, weight_ref, own, other, swap, stat_plane, stat_line,
    count_ref, first_ref, second_ref,
    local_sem, ring_send, ring_recv, spread_send, spread_recv, plane_send, plane_recv, small_send, small_recv,
):
    half, x, y, z = (lax.axis_index(name) for name in HALF_ROW_COL)
    in_plane, in_line = x * 4 + y, z * 2 + half
    place_plane = lambda peer: {"row_0": peer // 4, "row_1": peer % 4}
    place_line = lambda peer: {"col": peer // 2, "half": peer % 2}

    barrier = pltpu.get_barrier_semaphore()
    for me, place in ((in_plane, place_plane), (in_line, place_line)):
        for step in range(1, 16):
            pl.semaphore_signal(barrier, inc=1, device_id=place((me + step) % 16), device_id_type=MESH)
    loads = [
        pltpu.make_async_copy(source, target, local_sem.at[index])
        for index, (source, target) in enumerate(
            (
                (bin_hbm, bins),
                (slope_hbm, slopes),
                (table_hbm, table),
                (particle_hbm.at[0], data.at[0]),
                (particle_hbm.at[1], data.at[1]),
            )
        )
    ]
    for load in loads:
        load.start()
    loads[0].wait()
    loads[1].wait()
    lane = iota((1, 128), 1)
    info = jnp.zeros((1, 128), jnp.int32)
    for particle in range(2):
        info = jnp.where(lane == particle, bins[particle], info)
        for side in range(2):
            info = jnp.where(lane == 2 + 2 * particle + side, slopes[particle, side], info)
    info_ref[...] = info

    order = owner_rows(x, y)
    loads[2].wait()
    operators = [third_operator(table[bins[particle], 2]) for particle in range(2)]
    second = jnp.concatenate(
        [table[bins[particle], 1].astype(F32) for particle in range(2)], axis=1
    ).astype(BF16)
    for particle in range(2):
        loads[3 + particle].wait()
        along_first(particle, order, bins, slopes, data, table, first)

    pl.semaphore_wait(barrier, 30)
    gathered[half, z, in_plane] = info_ref[...]
    pending = exchange(
        in_plane, 16, place_plane, lambda peer: info_ref, gathered.at[half, z, in_plane], small_send.at[0], small_recv.at[0]
    )
    info_copies = list(pending)

    rings = [
        [
            Ring4(
                axis,
                lambda group, side, color=color, inner=inner: volume.at[group, color, inner, pl.ds(2 * side, 2)],
                ring_buffer.at[color, inner],
                ring_send.at[color, inner],
                ring_recv.at[color, inner],
            )
            for color, axis in enumerate(("row_0", "row_1"))
        ]
        for inner in range(2)
    ]
    flat = rings[0] + rings[1]
    group = functools.partial(
        insert_group,
        operators=operators, second=second, first=first, middles=(middle0, middle1), volume=volume,
    )
    group(0)
    for ring in flat:
        ring.send_far()
    group(1)
    for ring in flat:
        ring.send_right()
    group(2)
    for ring in flat:
        ring.send_left()
    arrived(info_copies)
    info_copies = exchange(
        in_line, 16, place_line, lambda peer: gathered.at[half, z], gathered.at[half, z], small_send.at[1], small_recv.at[1]
    )
    pending += info_copies
    group(3)
    for ring in rings[0]:
        ring.forward()
    arrived(info_copies)
    bin_counts([gathered[index].reshape(128, 128) for index in range(2)], count_ref)
    for ring in rings[1]:
        ring.forward()
    insert_counts(table, count_ref, first_ref, second_ref)

    own_plane = in_plane * 4 + half * 2
    spreads = []
    for inner in range(2):
        spreads.append([])
        for color, axis in enumerate(("row_1", "row_0")):
            rings[inner][color].finish(part.at[color, inner])
            me = lax.axis_index(axis)
            spreads[inner] += exchange(
                me,
                4,
                lambda peer, axis=axis: {axis: peer},
                lambda peer, color=color, inner=inner: part.at[color, inner, peer],
                spread_buffer.at[color, inner, me],
                spread_send.at[color, inner],
                spread_recv.at[color, inner],
            )
        if inner == 0:
            weight_sums(own_plane, z, table, first_ref, second_ref, weight_ref)
    plane_copies = []
    for inner in range(2):
        arrived(spreads[inner])
        pending += spreads[inner]
        for color, axis in enumerate(("row_1", "row_0")):
            me = lax.axis_index(axis)
            total = part[color, inner, me]
            for step in range(1, 4):
                total = total + spread_buffer[color, inner, (me + step) % 4]
            slab[color, inner] = total
        for core in range(2):
            for step in range(1 - core, 8):
                peer = (z + step) % 8
                target = half if core == 0 else 1 - half
                plane_copies.append(
                    remote(
                        slab.at[target, inner, pl.ds(pl.multiple_of(peer * 8, 8), 8)],
                        planes.at[half, inner, z],
                        plane_send.at[inner, core, step],
                        plane_recv.at[inner, core, step],
                        {"col": peer, "half": target},
                    )
                )
        planes[half, inner, z] = slab[half, inner, pl.ds(pl.multiple_of(z * 8, 8), 8)]
    arrived(plane_copies)
    pending += plane_copies

    maps = [[], []]
    for which in range(2):
        for inner in range(2):
            total = planes[which, inner, 0]
            for index in range(1, 8):
                total = total + planes[which, inner, index]
            maps[which].append(total / (weight_ref[which, inner] + 1.0))
            own[which, inner] = maps[which][inner]
    partner = remote(
        own.at[1 - half], other, small_send.at[4, 0], small_recv.at[4, 0], {"half": 1 - half}
    )
    stat_plane[in_plane] = shell_rows(maps[0], maps[1], own_plane, z)
    copies = exchange(
        in_plane, 16, place_plane, lambda peer: stat_plane.at[in_plane], stat_plane.at[in_plane], small_send.at[2], small_recv.at[2]
    )
    pending += copies
    partner.wait_recv()
    for inner in range(2):
        swap[half * 2 + inner] = own[half, inner]
        swap[(1 - half) * 2 + inner] = other[inner]
    low = iota((4, 128), 1) < 64
    for plane in range(4):
        even = swap[plane, pl.ds(0, 4, stride=2), :]
        odd = swap[plane, pl.ds(1, 4, stride=2), :]
        parts = (
            jnp.where(low, even, pltpu.roll(odd, 64, 1)),
            jnp.where(low, pltpu.roll(even, 64, 1), odd),
        )
        for component in range(2):
            for piece in range(4):
                map_ref[0, component, pl.ds(plane, 1), pl.ds(128 * piece, 128)] = parts[component][
                    piece : piece + 1
                ]
    arrived(copies)

    def summed(ref):
        total = ref[0]
        for index in range(1, 16):
            total = total + ref[index]
        return total

    stat_line[in_line] = summed(stat_plane)
    copies = exchange(
        in_line, 16, place_line, lambda peer: stat_line.at[in_line], stat_line.at[in_line], small_send.at[3], small_recv.at[3]
    )
    pending += copies
    arrived(copies)
    stat = jnp.broadcast_to(summed(stat_line), (8, 128))
    power_first, power_second, counts = (pltpu.roll(stat, 128 - 32 * kind, 1) for kind in (1, 2, 3))
    correlation = stat / jnp.sqrt(power_first * power_second + 1e-06)
    power_ref[pl.ds(0, 1), :] = (power_first / counts)[:1, :SHELLS]
    power_ref[pl.ds(1, 1), :] = (power_second / counts)[:1, :SHELLS]
    correlation_ref[...] = correlation[:1, :SHELLS]
    for ring in flat:
        pending += ring.copies
    pending.append(partner)
    for copy in pending:
        copy.wait_send()


def local(particles, orient_bin, tilt_slope, interp_table):
    hbm = pl.BlockSpec(memory_space=pltpu.HBM)
    vmem = pl.BlockSpec(memory_space=pltpu.VMEM)
    dma = pltpu.SemaphoreType.DMA
    f32 = lambda *shape: pltpu.VMEM(shape, F32)
    return pl.pallas_call(
        kernel,
        out_shape=(
            jax.ShapeDtypeStruct((1, 2, 4, 512), F32),
            jax.ShapeDtypeStruct((2, SHELLS), F32),
            jax.ShapeDtypeStruct((1, SHELLS), F32),
        ),
        in_specs=[hbm] * 4,
        out_specs=(vmem, vmem, vmem),
        scratch_shapes=[
            pltpu.VMEM((2, 2, GRID, GRID * GRID), BF16),
            pltpu.SMEM((2,), jnp.int32),
            pltpu.SMEM((2, 2), jnp.int32),
            pltpu.VMEM((BINS, 3, GRID, GRID), BF16),
            pltpu.VMEM((2, 32, GRID, 256), BF16),
            f32(GRID * STRIDE, 128),
            f32(GRID * STRIDE, 128),
            f32(4, 2, 2, 4, GRID, 128),
            f32(2, 2, 6, 2, GRID, 128),
            f32(2, 2, 4, GRID, 128),
            f32(2, 2, 4, GRID, 128),
            f32(2, 2, GRID, 128),
            f32(2, 2, 8, 8, 128),
            pltpu.VMEM((1, 128), jnp.int32),
            pltpu.VMEM((2, 8, 16, 1, 128), jnp.int32),
            f32(2, 2, 8, 128),
            f32(2, 2, 8, 128),
            f32(2, 8, 128),
            f32(4, 8, 128),
            f32(16, 1, 128),
            f32(16, 1, 128),
            f32(GRID * 2 * BINS, 128),
            f32(2, BINS, GRID, 128),
            f32(GRID, 128),
            dma((5,)),
            dma((2, 2, 6)),
            dma((2, 2, 6)),
            dma((2, 2, 4)),
            dma((2, 2, 4)),
            dma((2, 2, 8)),
            dma((2, 2, 8)),
            dma((5, 16)),
            dma((5, 16)),
        ],
        compiler_params=pltpu.CompilerParams(
            collective_id=0, has_side_effects=True, vmem_limit_bytes=60 * 2**20
        ),
        name="halfmaps",
    )(particles, orient_bin, tilt_slope, interp_table)


def solution(mesh):
    torus = Mesh(
        mesh.devices.reshape(mesh.shape["half"], 4, 4, mesh.shape["col"]), HALF_ROW_COL
    )
    in_specs = (P(HALF_ROW_COL, None, None, None), P(HALF_ROW_COL), P(HALF_ROW_COL, None), P())
    out_specs = (P("half", None, ("row_0", "row_1"), "col"), P(), P("half", None))
    return jax.shard_map(local, mesh=torus, in_specs=in_specs, out_specs=out_specs, check_vma=False)
```

time: 171 us -> 57.3 us (0.34)
  the two profiles are of different devices: /device:TPU:2 before, /device:TPU:1 now
where the time goes in v2:
time: 57.3 us; the launch traced here: 57.1 us
  Pallas kernels  52.7 us (92%)
  local copies, waits for them, and re-layouts  3.72 us (6%)
  between operations  0.64 us (1%)
    pallas_call x1, Pallas kernels, local(): pl.pallas_call(kernel, out_shape=(jax.ShapeDtypeStruct((1, 2, 4, 512), F3...  52.7 us
    unnamed x3, local copies, waits for them, and re-layouts  3.72 us

profile of v2, /device:TPU:1, one launch (start us, length us, event | category | flops | bytes accessed | tf_op | source)
XLA Modules:
  0.0 57.1 jit_solution(11918265316925219175)
XLA Ops:
  0.6 52.7 %halfmaps.1 = (f32[1,2,4,512]{3,2,1,0:T(4,128)}, f32[2,29]{1,0:T(2,128)}, f32[1,29]{1,0:T(1,128)}) custom-call(bf16[2,2,64,4096]{3,2,1,0:T(8,128)(2,1)} %particle_hbm.1, s32[2]{0:T(128)} %bin_hbm.1, s32[2,2]{1,0:T(2,128)} %slope_hbm.1, bf16[16,3,64,64]{3,2,1,0:T(8,128)(2,1)} %table_hbm.1), custom_call_target="tpu_custom_call" | custom-call | tf_op jit(solution)/shard_map/halfmaps/pallas_call | solution.py:454
  53.3 1.3 %copy.10 = f32[1,2,4,512]{3,2,1,0:T(4,128)} copy(f32[1,2,4,512]{3,2,1,0:T(4,128)} %get-tuple-element.6) | data formatting | bytes 32768
  54.7 1.2 %copy.11 = f32[2,29]{1,0:T(2,128)} copy(f32[2,29]{1,0:T(2,128)} %get-tuple-element.7) | data formatting | bytes 464
  55.9 1.2 %copy.12 = f32[1,29]{1,0:T(1,128)} copy(f32[1,29]{1,0:T(1,128)} %get-tuple-element.8) | data formatting | bytes 232

commit v3 on v2

--- a/solution.py
+++ b/solution.py
@@ -1,4 +1,5 @@
 import functools
+import itertools
 
 import jax
 import jax.numpy as jnp
@@ -12,6 +13,7 @@
 GRID = 64
 BINS = 16
 STRIDE = 24
+SIZES = {"half": 2, "row_0": 4, "row_1": 4, "col": 8}
 HALF_ROW_COL = ("half", "row_0", "row_1", "col")
 MESH = pl.DeviceIdType.MESH
 F32 = jnp.float32
@@ -80,42 +82,46 @@
 
 
 def bin_counts(infos, count_ref):
-    lane = iota((128, 128), 1)
-    histograms = []
+    contract = functools.partial(
+        lax.dot_general, dimension_numbers=(((1,), (1,)), ((), ())), preferred_element_type=F32
+    )
+    bin_index = iota((BINS, 128), 0).astype(F32)
+    slope_index = iota((GRID, 128), 0).astype(F32)
+    parts = [[], []]
     for info in infos:
-        bins, slopes = [], []
-        for particle in range(2):
-            bins.append((info[:, particle : particle + 1] == lane).astype(F32))
-            limit = jnp.where(
-                lane < 64,
-                info[:, 2 + 2 * particle : 3 + 2 * particle],
-                info[:, 3 + 2 * particle : 4 + 2 * particle],
-            )
-            slopes.append((limit == (lane & 63)).astype(F32))
-        bins = jnp.concatenate([jnp.transpose(part)[:BINS] for part in bins], axis=1).astype(BF16)
-        slopes = jnp.concatenate(slopes, axis=0).astype(BF16)
-        histograms.append(jnp.dot(bins, slopes, preferred_element_type=F32))
-    histogram = jnp.concatenate(histograms, axis=0).astype(BF16)
-
-    wave_third = (iota((128, 128), 1) & 63) - 32
-    reach = (16 * jnp.abs(wave_third)).astype(F32)
-    limit = (iota((128, 128), 0) & 63).astype(F32)
-    same_side = iota((128, 128), 0) < 64
-    nonneg_third, nonpos_third = wave_third >= 0, wave_third <= 0
+        fields = jnp.transpose(info.astype(F32))[:8]
+        bins = [(fields[particle : particle + 1] == bin_index).astype(F32) for particle in range(2)]
+        bins = jnp.concatenate(bins, axis=1).astype(BF16)
+        for side in range(2):
+            slopes = [
+                (fields[2 + 2 * particle + side : 3 + 2 * particle + side] == slope_index).astype(F32)
+                for particle in range(2)
+            ]
+            parts[side].append(contract(bins, jnp.concatenate(slopes, axis=1).astype(BF16)))
+    histogram = jnp.concatenate(parts[0] + parts[1], axis=0).astype(BF16)
+
+    reach = (16 * jnp.abs((iota((GRID, 128), 1) & 63) - 32)).astype(F32)
+    wave_third = (iota((2 * BINS, 128), 1) & 63) - 32
+    nonneg, nonpos = wave_third >= 0, wave_third <= 0
+
+    def counted(distance):
+        inside = (reach <= slope_index * distance).astype(F32).astype(BF16)
+        counts = jnp.dot(histogram, inside, preferred_element_type=F32)
+        return counts[: 2 * BINS], counts[2 * BINS :]
+
+    def place(first):
+        return pl.ds(pl.multiple_of(first * 2 * BINS, 2 * BINS), 2 * BINS)
 
     def planes(step, carry):
-        for inner in range(4):
-            first = step * 4 + inner
-            wave_first = first - 32
-            agree = (
-                ((wave_first > 0) & nonneg_third) | ((wave_first < 0) & nonpos_third) | (wave_first == 0)
-            )
-            inside = (reach <= limit * jnp.abs(wave_first).astype(F32)) & (agree == same_side)
-            counts = jnp.dot(histogram, inside.astype(F32).astype(BF16), preferred_element_type=F32)
-            count_ref[pl.ds(pl.multiple_of(first * 2 * BINS, 2 * BINS), 2 * BINS), :] = counts
+        for inner in range(8):
+            distance = step * 8 + inner + 1
+            same, opposite = counted(distance.astype(F32))
+            count_ref[place(32 + distance), :] = jnp.where(nonneg, same, opposite)
+            count_ref[place(32 - distance), :] = jnp.where(nonpos, same, opposite)
         return carry
 
-    lax.fori_loop(0, GRID // 4, planes, 0)
+    count_ref[place(32), :] = counted(0.0)[0]
+    lax.fori_loop(0, 4, planes, 0)
 
 
 def insert_counts(table, count_ref, first_ref, second_ref):
@@ -197,12 +203,25 @@
             )
 
 
-def exchange(me, size, place, source, target, send, recv):
-    copies = []
-    for step in range(1, size):
-        peer = (me + step) % size
-        copies.append(remote(source(peer), target, send.at[step], recv.at[step], place(peer)))
-    return copies
+def hops(offset, sizes):
+    return sum(min(step, size - step) for step, size in zip(offset, sizes))
+
+
+def others(*axes):
+    sizes = [SIZES[axis] for axis in axes]
+    offsets = [offset for offset in itertools.product(*map(range, sizes)) if any(offset)]
+    offsets.sort(key=lambda offset: -hops(offset, sizes))
+    places = {
+        axis: [lax.rem(lax.axis_index(axis) + step, size) for step in range(size)]
+        for axis, size in zip(axes, sizes)
+    }
+    return [{axis: places[axis][step] for axis, step in zip(axes, offset)} for offset in offsets]
+
+
+def exchange(peers, source, target, send, recv):
+    return [
+        remote(source(peer), target, send.at[index], recv.at[index], peer) for index, peer in enumerate(peers)
+    ]
 
 
 def arrived(copies):
@@ -252,13 +271,6 @@
 ):
     half, x, y, z = (lax.axis_index(name) for name in HALF_ROW_COL)
     in_plane, in_line = x * 4 + y, z * 2 + half
-    place_plane = lambda peer: {"row_0": peer // 4, "row_1": peer % 4}
-    place_line = lambda peer: {"col": peer // 2, "half": peer % 2}
-
-    barrier = pltpu.get_barrier_semaphore()
-    for me, place in ((in_plane, place_plane), (in_line, place_line)):
-        for step in range(1, 16):
-            pl.semaphore_signal(barrier, inc=1, device_id=place((me + step) % 16), device_id_type=MESH)
     loads = [
         pltpu.make_async_copy(source, target, local_sem.at[index])
         for index, (source, target) in enumerate(
@@ -273,6 +285,10 @@
     ]
     for load in loads:
         load.start()
+    plane_peers, line_peers = others("row_0", "row_1"), others("col", "half")
+    barrier = pltpu.get_barrier_semaphore()
+    for peer in plane_peers + line_peers:
+        pl.semaphore_signal(barrier, inc=1, device_id=peer, device_id_type=MESH)
     loads[0].wait()
     loads[1].wait()
     lane = iota((1, 128), 1)
@@ -292,13 +308,6 @@
     for particle in range(2):
         loads[3 + particle].wait()
         along_first(particle, order, bins, slopes, data, table, first)
-
-    pl.semaphore_wait(barrier, 30)
-    gathered[half, z, in_plane] = info_ref[...]
-    pending = exchange(
-        in_plane, 16, place_plane, lambda peer: info_ref, gathered.at[half, z, in_plane], small_send.at[0], small_recv.at[0]
-    )
-    info_copies = list(pending)
 
     rings = [
         [
@@ -319,6 +328,12 @@
         operators=operators, second=second, first=first, middles=(middle0, middle1), volume=volume,
     )
     group(0)
+    pl.semaphore_wait(barrier, 30)
+    gathered[half, z, in_plane] = info_ref[...]
+    info_copies = exchange(
+        plane_peers, lambda peer: info_ref, gathered.at[half, z, in_plane], small_send.at[0], small_recv.at[0]
+    )
+    pending = list(info_copies)
     for ring in flat:
         ring.send_far()
     group(1)
@@ -329,7 +344,7 @@
         ring.send_left()
     arrived(info_copies)
     info_copies = exchange(
-        in_line, 16, place_line, lambda peer: gathered.at[half, z], gathered.at[half, z], small_send.at[1], small_recv.at[1]
+        line_peers, lambda peer: gathered.at[half, z], gathered.at[half, z], small_send.at[1], small_recv.at[1]
     )
     pending += info_copies
     group(3)
@@ -349,10 +364,8 @@
             rings[inner][color].finish(part.at[color, inner])
             me = lax.axis_index(axis)
             spreads[inner] += exchange(
-                me,
-                4,
-                lambda peer, axis=axis: {axis: peer},
-                lambda peer, color=color, inner=inner: part.at[color, inner, peer],
+                others(axis),
+                lambda peer, axis=axis, color=color, inner=inner: part.at[color, inner, peer[axis]],
                 spread_buffer.at[color, inner, me],
                 spread_send.at[color, inner],
                 spread_recv.at[color, inner],
@@ -369,19 +382,15 @@
             for step in range(1, 4):
                 total = total + spread_buffer[color, inner, (me + step) % 4]
             slab[color, inner] = total
-        for core in range(2):
-            for step in range(1 - core, 8):
-                peer = (z + step) % 8
-                target = half if core == 0 else 1 - half
-                plane_copies.append(
-                    remote(
-                        slab.at[target, inner, pl.ds(pl.multiple_of(peer * 8, 8), 8)],
-                        planes.at[half, inner, z],
-                        plane_send.at[inner, core, step],
-                        plane_recv.at[inner, core, step],
-                        {"col": peer, "half": target},
-                    )
-                )
+        plane_copies += exchange(
+            line_peers,
+            lambda peer, inner=inner: slab.at[
+                peer["half"], inner, pl.ds(pl.multiple_of(peer["col"] * 8, 8), 8)
+            ],
+            planes.at[half, inner, z],
+            plane_send.at[inner],
+            plane_recv.at[inner],
+        )
         planes[half, inner, z] = slab[half, inner, pl.ds(pl.multiple_of(z * 8, 8), 8)]
     arrived(plane_copies)
     pending += plane_copies
@@ -399,7 +408,7 @@
     )
     stat_plane[in_plane] = shell_rows(maps[0], maps[1], own_plane, z)
     copies = exchange(
-        in_plane, 16, place_plane, lambda peer: stat_plane.at[in_plane], stat_plane.at[in_plane], small_send.at[2], small_recv.at[2]
+        plane_peers, lambda peer: stat_plane.at[in_plane], stat_plane.at[in_plane], small_send.at[2], small_recv.at[2]
     )
     pending += copies
     partner.wait_recv()
@@ -429,7 +438,7 @@
 
     stat_line[in_line] = summed(stat_plane)
     copies = exchange(
-        in_line, 16, place_line, lambda peer: stat_line.at[in_line], stat_line.at[in_line], small_send.at[3], small_recv.at[3]
+        line_peers, lambda peer: stat_line.at[in_line], stat_line.at[in_line], small_send.at[3], small_recv.at[3]
     )
     pending += copies
     arrived(copies)
@@ -446,18 +455,30 @@
         copy.wait_send()
 
 
+def emit_kernel(map_ref, power_ref, correlation_ref, map_out, power_out, correlation_out, sems):
+    pairs = ((map_ref, map_out), (power_ref, power_out), (correlation_ref, correlation_out))
+    copies = [
+        pltpu.make_async_copy(source, target, sems.at[index]) for index, (source, target) in enumerate(pairs)
+    ]
+    for copy in copies:
+        copy.start()
+    for copy in copies:
+        copy.wait()
+
+
 def local(particles, orient_bin, tilt_slope, interp_table):
     hbm = pl.BlockSpec(memory_space=pltpu.HBM)
     vmem = pl.BlockSpec(memory_space=pltpu.VMEM)
     dma = pltpu.SemaphoreType.DMA
     f32 = lambda *shape: pltpu.VMEM(shape, F32)
-    return pl.pallas_call(
+    shapes = (
+        jax.ShapeDtypeStruct((1, 2, 4, 512), F32),
+        jax.ShapeDtypeStruct((2, SHELLS), F32),
+        jax.ShapeDtypeStruct((1, SHELLS), F32),
+    )
+    results = pl.pallas_call(
         kernel,
-        out_shape=(
-            jax.ShapeDtypeStruct((1, 2, 4, 512), F32),
-            jax.ShapeDtypeStruct((2, SHELLS), F32),
-            jax.ShapeDtypeStruct((1, SHELLS), F32),
-        ),
+        out_shape=tuple(pltpu.VMEM(shape.shape, F32) for shape in shapes),
         in_specs=[hbm] * 4,
         out_specs=(vmem, vmem, vmem),
         scratch_shapes=[
@@ -482,7 +503,7 @@
             f32(4, 8, 128),
             f32(16, 1, 128),
             f32(16, 1, 128),
-            f32(GRID * 2 * BINS, 128),
+            f32((GRID + 1) * 2 * BINS, 128),
             f32(2, BINS, GRID, 128),
             f32(GRID, 128),
             dma((5,)),
@@ -490,8 +511,8 @@
             dma((2, 2, 6)),
             dma((2, 2, 4)),
             dma((2, 2, 4)),
-            dma((2, 2, 8)),
-            dma((2, 2, 8)),
+            dma((2, 16)),
+            dma((2, 16)),
             dma((5, 16)),
             dma((5, 16)),
         ],
@@ -500,6 +521,15 @@
         ),
         name="halfmaps",
     )(particles, orient_bin, tilt_slope, interp_table)
+    return pl.pallas_call(
+        emit_kernel,
+        out_shape=shapes,
+        in_specs=[vmem] * 3,
+        out_specs=(hbm,) * 3,
+        scratch_shapes=[dma((3,))],
+        compiler_params=pltpu.CompilerParams(vmem_limit_bytes=2**20),
+        name="emit",
+    )(*results)
 
 
 def solution(mesh):

time: 57.3 us -> 48.5 us (0.85)
  Pallas kernels: 52.7 us -> 47.8 us
  local copies, waits for them, and re-layouts: 3.72 us -> 0 us
    pallas_call x1 -> x2, Pallas kernels: 52.7 us -> 47.8 us  [the longest x1 47.1 us: local(): pl.pallas_call(kernel, out_shape=tuple((pltpu.VMEM(shape.shape, F32) for...]
    unnamed x3 -> x0, local copies, waits for them, and re-layouts: 3.72 us -> none
where the time goes in v3:
time: 48.5 us; the launch traced here: 48.4 us
  Pallas kernels  47.8 us (99%)
  between operations  0.64 us (1%)
    pallas_call x1, Pallas kernels, local(): pl.pallas_call(kernel, out_shape=tuple((pltpu.VMEM(shape.shape, F32) for...  47.1 us

profile of v3, /device:TPU:1, one launch (start us, length us, event | category | flops | bytes accessed | tf_op | source)
XLA Modules:
  0.0 48.4 jit_solution(15321108009971000501)
XLA Ops:
  0.6 47.1 %halfmaps.1 = (f32[1,2,4,512]{3,2,1,0:T(4,128)S(1)}, f32[2,29]{1,0:T(2,128)S(1)}, f32[1,29]{1,0:T(1,128)S(1)}) custom-call(bf16[2,2,64,4096]{3,2,1,0:T(8,128)(2,1)} %particle_hbm.1, s32[2]{0:T(128)} %bin_hbm.1, s32[2,2]{1,0:T(2,128)} %slope_hbm.1, bf16[16,3,64,64]{3,2,1,0:T(8,128)(2,1)} %table_hbm.1), custom_call_target="tpu_custom_call" | custom-call | tf_op jit(solution)/shard_map/halfmaps/pallas_call | solution.py:479
  47.8 0.6 %emit.1 = (f32[1,2,4,512]{3,2,1,0:T(4,128)}, f32[2,29]{1,0:T(2,128)}, f32[1,29]{1,0:T(1,128)}) custom-call(f32[1,2,4,512]{3,2,1,0:T(4,128)S(1)} %get-tuple-element.6.map_ref, f32[2,29]{1,0:T(2,128)S(1)} %get-tuple-element.7.power_ref, f32[1,29]{1,0:T(1,128)S(1)} %get-tuple-element.8.correlation_ref), custom_call_target="tpu_custom_call" | custom-call | tf_op jit(solution)/shard_map/emit/pallas_call | solution.py:524

commit v4 on v3

--- a/solution.py
+++ b/solution.py
@@ -342,19 +342,14 @@
     group(2)
     for ring in flat:
         ring.send_left()
+    group(3)
+    for ring in flat:
+        ring.forward()
     arrived(info_copies)
     info_copies = exchange(
         line_peers, lambda peer: gathered.at[half, z], gathered.at[half, z], small_send.at[1], small_recv.at[1]
     )
     pending += info_copies
-    group(3)
-    for ring in rings[0]:
-        ring.forward()
-    arrived(info_copies)
-    bin_counts([gathered[index].reshape(128, 128) for index in range(2)], count_ref)
-    for ring in rings[1]:
-        ring.forward()
-    insert_counts(table, count_ref, first_ref, second_ref)
 
     own_plane = in_plane * 4 + half * 2
     spreads = []
@@ -370,8 +365,6 @@
                 spread_send.at[color, inner],
                 spread_recv.at[color, inner],
             )
-        if inner == 0:
-            weight_sums(own_plane, z, table, first_ref, second_ref, weight_ref)
     plane_copies = []
     for inner in range(2):
         arrived(spreads[inner])
@@ -392,6 +385,12 @@
             plane_recv.at[inner],
         )
         planes[half, inner, z] = slab[half, inner, pl.ds(pl.multiple_of(z * 8, 8), 8)]
+        if inner == 0:
+            arrived(info_copies)
+            bin_counts([gathered[index].reshape(128, 128) for index in range(2)], count_ref)
+            insert_counts(table, count_ref, first_ref, second_ref)
+        else:
+            weight_sums(own_plane, z, table, first_ref, second_ref, weight_ref)
     arrived(plane_copies)
     pending += plane_copies
 

time: 48.5 us -> 45.9 us (0.946)
  Pallas kernels: 47.8 us -> 45.2 us
    pallas_call x1, Pallas kernels: 47.1 us -> 44.5 us  [local(): pl.pallas_call(kernel, out_shape=tuple((pltpu.VMEM(shape.shape, F32) for...]
where the time goes in v4:
time: 45.9 us; the launch traced here: 45.8 us
  Pallas kernels  45.2 us (98%)
  between operations  0.64 us (1%)
    pallas_call x1, Pallas kernels, local(): pl.pallas_call(kernel, out_shape=tuple((pltpu.VMEM(shape.shape, F32) for...  44.5 us

profile of v4, /device:TPU:1, one launch (start us, length us, event | category | flops | bytes accessed | tf_op | source)
XLA Modules:
  0.0 45.8 jit_solution(43939133017125717)
XLA Ops:
  0.6 44.5 %halfmaps.1 = (f32[1,2,4,512]{3,2,1,0:T(4,128)S(1)}, f32[2,29]{1,0:T(2,128)S(1)}, f32[1,29]{1,0:T(1,128)S(1)}) custom-call(bf16[2,2,64,4096]{3,2,1,0:T(8,128)(2,1)} %particle_hbm.1, s32[2]{0:T(128)} %bin_hbm.1, s32[2,2]{1,0:T(2,128)} %slope_hbm.1, bf16[16,3,64,64]{3,2,1,0:T(8,128)(2,1)} %table_hbm.1), custom_call_target="tpu_custom_call" | custom-call | tf_op jit(solution)/shard_map/halfmaps/pallas_call | solution.py:478
  45.2 0.6 %emit.1 = (f32[1,2,4,512]{3,2,1,0:T(4,128)}, f32[2,29]{1,0:T(2,128)}, f32[1,29]{1,0:T(1,128)}) custom-call(f32[1,2,4,512]{3,2,1,0:T(4,128)S(1)} %get-tuple-element.6.map_ref, f32[2,29]{1,0:T(2,128)S(1)} %get-tuple-element.7.power_ref, f32[1,29]{1,0:T(1,128)S(1)} %get-tuple-element.8.correlation_ref), custom_call_target="tpu_custom_call" | custom-call | tf_op jit(solution)/shard_map/emit/pallas_call | solution.py:523

commit v5 on v4

--- a/solution.py
+++ b/solution.py
@@ -265,9 +265,9 @@
 def kernel(
     particle_hbm, bin_hbm, slope_hbm, table_hbm, map_ref, power_ref, correlation_ref,
     data, bins, slopes, table, first, middle0, middle1, volume,
-    ring_buffer, part, spread_buffer, slab, planes, info_ref, gathered, weight_ref, own, other, swap, stat_plane, stat_line,
+    ring_buffer, part, spread_buffer, slab, planes, info_ref, gathered, weight_ref, own, other, swap, stat_all,
     count_ref, first_ref, second_ref,
-    local_sem, ring_send, ring_recv, spread_send, spread_recv, plane_send, plane_recv, small_send, small_recv,
+    local_sem, ring_send, ring_recv, spread_send, spread_recv, plane_send, plane_recv, small_send, small_recv, stat_sem,
 ):
     half, x, y, z = (lax.axis_index(name) for name in HALF_ROW_COL)
     in_plane, in_line = x * 4 + y, z * 2 + half
@@ -405,11 +405,12 @@
     partner = remote(
         own.at[1 - half], other, small_send.at[4, 0], small_recv.at[4, 0], {"half": 1 - half}
     )
-    stat_plane[in_plane] = shell_rows(maps[0], maps[1], own_plane, z)
-    copies = exchange(
-        plane_peers, lambda peer: stat_plane.at[in_plane], stat_plane.at[in_plane], small_send.at[2], small_recv.at[2]
-    )
-    pending += copies
+    everyone = others("half", "row_0", "row_1", "col")
+    me = (in_plane * 8 + z) * 2 + half
+    stat_all[me] = shell_rows(maps[0], maps[1], own_plane, z)
+    copies = [
+        remote(stat_all.at[me], stat_all.at[me], stat_sem.at[0], stat_sem.at[1], peer) for peer in everyone
+    ]
     partner.wait_recv()
     for inner in range(2):
         swap[half * 2 + inner] = own[half, inner]
@@ -427,21 +428,14 @@
                 map_ref[0, component, pl.ds(plane, 1), pl.ds(128 * piece, 128)] = parts[component][
                     piece : piece + 1
                 ]
-    arrived(copies)
-
-    def summed(ref):
-        total = ref[0]
-        for index in range(1, 16):
-            total = total + ref[index]
-        return total
-
-    stat_line[in_line] = summed(stat_plane)
-    copies = exchange(
-        line_peers, lambda peer: stat_line.at[in_line], stat_line.at[in_line], small_send.at[3], small_recv.at[3]
-    )
-    pending += copies
-    arrived(copies)
-    stat = jnp.broadcast_to(summed(stat_line), (8, 128))
+    whole = stat_all.at[pl.ds(0, len(copies))]
+    pltpu.make_async_copy(whole, whole, stat_sem.at[1]).wait()
+    totals = [stat_all[index] for index in range(8)]
+    for index in range(8, 256):
+        totals[index % 8] = totals[index % 8] + stat_all[index]
+    while len(totals) > 1:
+        totals = [first + second for first, second in zip(totals[::2], totals[1::2])]
+    stat = jnp.broadcast_to(totals[0], (8, 128))
     power_first, power_second, counts = (pltpu.roll(stat, 128 - 32 * kind, 1) for kind in (1, 2, 3))
     correlation = stat / jnp.sqrt(power_first * power_second + 1e-06)
     power_ref[pl.ds(0, 1), :] = (power_first / counts)[:1, :SHELLS]
@@ -452,6 +446,7 @@
     pending.append(partner)
     for copy in pending:
         copy.wait_send()
+    pltpu.make_async_copy(whole, whole, stat_sem.at[0]).wait()
 
 
 def emit_kernel(map_ref, power_ref, correlation_ref, map_out, power_out, correlation_out, sems):
@@ -500,8 +495,7 @@
             f32(2, 2, 8, 128),
             f32(2, 8, 128),
             f32(4, 8, 128),
-            f32(16, 1, 128),
-            f32(16, 1, 128),
+            f32(256, 1, 128),
             f32((GRID + 1) * 2 * BINS, 128),
             f32(2, BINS, GRID, 128),
             f32(GRID, 128),
@@ -514,6 +508,7 @@
             dma((2, 16)),
             dma((5, 16)),
             dma((5, 16)),
+            dma((2,)),
         ],
         compiler_params=pltpu.CompilerParams(
             collective_id=0, has_side_effects=True, vmem_limit_bytes=60 * 2**20

time: 45.9 us -> 44.1 us (0.961)
  Pallas kernels: 45.2 us -> 43.4 us
    pallas_call x1, Pallas kernels: 44.5 us -> 42.8 us  [local(): pl.pallas_call(kernel, out_shape=tuple((pltpu.VMEM(shape.shape, F32) for...]
where the time goes in v5:
time: 44.1 us; the launch traced here: 44 us
  Pallas kernels  43.4 us (98%)
  between operations  0.64 us (1%)
    pallas_call x1, Pallas kernels, local(): pl.pallas_call(kernel, out_shape=tuple((pltpu.VMEM(shape.shape, F32) for...  42.8 us

profile of v5, /device:TPU:1, one launch (start us, length us, event | category | flops | bytes accessed | tf_op | source)
XLA Modules:
  0.0 44.0 jit_solution(10497937779411090354)
XLA Ops:
  0.6 42.8 %halfmaps.1 = (f32[1,2,4,512]{3,2,1,0:T(4,128)S(1)}, f32[2,29]{1,0:T(2,128)S(1)}, f32[1,29]{1,0:T(1,128)S(1)}) custom-call(bf16[2,2,64,4096]{3,2,1,0:T(8,128)(2,1)} %particle_hbm.1, s32[2]{0:T(128)} %bin_hbm.1, s32[2,2]{1,0:T(2,128)} %slope_hbm.1, bf16[16,3,64,64]{3,2,1,0:T(8,128)(2,1)} %table_hbm.1), custom_call_target="tpu_custom_call" | custom-call | tf_op jit(solution)/shard_map/halfmaps/pallas_call | solution.py:473
  43.4 0.6 %emit.1 = (f32[1,2,4,512]{3,2,1,0:T(4,128)}, f32[2,29]{1,0:T(2,128)}, f32[1,29]{1,0:T(1,128)}) custom-call(f32[1,2,4,512]{3,2,1,0:T(4,128)S(1)} %get-tuple-element.6.map_ref, f32[2,29]{1,0:T(2,128)S(1)} %get-tuple-element.7.power_ref, f32[1,29]{1,0:T(1,128)S(1)} %get-tuple-element.8.correlation_ref), custom_call_target="tpu_custom_call" | custom-call | tf_op jit(solution)/shard_map/emit/pallas_call | solution.py:518

commit v6 on v5

--- a/solution.py
+++ b/solution.py
@@ -375,31 +375,27 @@
             for step in range(1, 4):
                 total = total + spread_buffer[color, inner, (me + step) % 4]
             slab[color, inner] = total
-        plane_copies += exchange(
-            line_peers,
-            lambda peer, inner=inner: slab.at[
-                peer["half"], inner, pl.ds(pl.multiple_of(peer["col"] * 8, 8), 8)
-            ],
-            planes.at[half, inner, z],
-            plane_send.at[inner],
-            plane_recv.at[inner],
-        )
-        planes[half, inner, z] = slab[half, inner, pl.ds(pl.multiple_of(z * 8, 8), 8)]
-        if inner == 0:
-            arrived(info_copies)
-            bin_counts([gathered[index].reshape(128, 128) for index in range(2)], count_ref)
-            insert_counts(table, count_ref, first_ref, second_ref)
-        else:
-            weight_sums(own_plane, z, table, first_ref, second_ref, weight_ref)
+    plane_copies = exchange(
+        line_peers,
+        lambda peer: slab.at[peer["half"], :, pl.ds(pl.multiple_of(peer["col"] * 8, 8), 8)],
+        planes.at[half, z],
+        plane_send.at[0],
+        plane_recv.at[0],
+    )
+    planes[half, z] = slab[half, :, pl.ds(pl.multiple_of(z * 8, 8), 8)]
+    arrived(info_copies)
+    bin_counts([gathered[index].reshape(128, 128) for index in range(2)], count_ref)
+    insert_counts(table, count_ref, first_ref, second_ref)
+    weight_sums(own_plane, z, table, first_ref, second_ref, weight_ref)
     arrived(plane_copies)
     pending += plane_copies
 
     maps = [[], []]
     for which in range(2):
         for inner in range(2):
-            total = planes[which, inner, 0]
+            total = planes[which, 0, inner]
             for index in range(1, 8):
-                total = total + planes[which, inner, index]
+                total = total + planes[which, index, inner]
             maps[which].append(total / (weight_ref[which, inner] + 1.0))
             own[which, inner] = maps[which][inner]
     partner = remote(
@@ -428,6 +424,11 @@
                 map_ref[0, component, pl.ds(plane, 1), pl.ds(128 * piece, 128)] = parts[component][
                     piece : piece + 1
                 ]
+    for ring in flat:
+        pending += ring.copies
+    pending.append(partner)
+    for copy in pending:
+        copy.wait_send()
     whole = stat_all.at[pl.ds(0, len(copies))]
     pltpu.make_async_copy(whole, whole, stat_sem.at[1]).wait()
     totals = [stat_all[index] for index in range(8)]
@@ -441,11 +442,6 @@
     power_ref[pl.ds(0, 1), :] = (power_first / counts)[:1, :SHELLS]
     power_ref[pl.ds(1, 1), :] = (power_second / counts)[:1, :SHELLS]
     correlation_ref[...] = correlation[:1, :SHELLS]
-    for ring in flat:
-        pending += ring.copies
-    pending.append(partner)
-    for copy in pending:
-        copy.wait_send()
     pltpu.make_async_copy(whole, whole, stat_sem.at[0]).wait()
 
 
@@ -488,7 +484,7 @@
             f32(2, 2, 4, GRID, 128),
             f32(2, 2, 4, GRID, 128),
             f32(2, 2, GRID, 128),
-            f32(2, 2, 8, 8, 128),
+            f32(2, 8, 2, 8, 128),
             pltpu.VMEM((1, 128), jnp.int32),
             pltpu.VMEM((2, 8, 16, 1, 128), jnp.int32),
             f32(2, 2, 8, 128),

time: 44.1 us -> 42.9 us (0.973)
  Pallas kernels: 43.4 us -> 42.1 us
    pallas_call x1, Pallas kernels: 42.8 us -> 41.5 us  [local(): pl.pallas_call(kernel, out_shape=tuple((pltpu.VMEM(shape.shape, F32) for...]
where the time goes in v6:
time: 42.9 us; the launch traced here: 42.7 us
  Pallas kernels  42.1 us (98%)
  between operations  0.64 us (1%)
    pallas_call x1, Pallas kernels, local(): pl.pallas_call(kernel, out_shape=tuple((pltpu.VMEM(shape.shape, F32) for...  41.5 us

profile of v6, /device:TPU:1, one launch (start us, length us, event | category | flops | bytes accessed | tf_op | source)
XLA Modules:
  0.0 42.7 jit_solution(16208241766884472437)
XLA Ops:
  0.6 41.5 %halfmaps.1 = (f32[1,2,4,512]{3,2,1,0:T(4,128)S(1)}, f32[2,29]{1,0:T(2,128)S(1)}, f32[1,29]{1,0:T(1,128)S(1)}) custom-call(bf16[2,2,64,4096]{3,2,1,0:T(8,128)(2,1)} %particle_hbm.1, s32[2]{0:T(128)} %bin_hbm.1, s32[2,2]{1,0:T(2,128)} %slope_hbm.1, bf16[16,3,64,64]{3,2,1,0:T(8,128)(2,1)} %table_hbm.1), custom_call_target="tpu_custom_call" | custom-call | tf_op jit(solution)/shard_map/halfmaps/pallas_call | solution.py:469
  42.1 0.6 %emit.1 = (f32[1,2,4,512]{3,2,1,0:T(4,128)}, f32[2,29]{1,0:T(2,128)}, f32[1,29]{1,0:T(1,128)}) custom-call(f32[1,2,4,512]{3,2,1,0:T(4,128)S(1)} %get-tuple-element.6.map_ref, f32[2,29]{1,0:T(2,128)S(1)} %get-tuple-element.7.power_ref, f32[1,29]{1,0:T(1,128)S(1)} %get-tuple-element.8.correlation_ref), custom_call_target="tpu_custom_call" | custom-call | tf_op jit(solution)/shard_map/emit/pallas_call | solution.py:514

commit v7 on v6

--- a/solution.py
+++ b/solution.py
@@ -267,7 +267,7 @@
     data, bins, slopes, table, first, middle0, middle1, volume,
     ring_buffer, part, spread_buffer, slab, planes, info_ref, gathered, weight_ref, own, other, swap, stat_all,
     count_ref, first_ref, second_ref,
-    local_sem, ring_send, ring_recv, spread_send, spread_recv, plane_send, plane_recv, small_send, small_recv, stat_sem,
+    local_sem, ring_send, ring_recv, spread_send, spread_recv, plane_send, plane_recv, small_send, small_recv, stat_sem, relay_sem,
 ):
     half, x, y, z = (lax.axis_index(name) for name in HALF_ROW_COL)
     in_plane, in_line = x * 4 + y, z * 2 + half
@@ -285,9 +285,11 @@
     ]
     for load in loads:
         load.start()
-    plane_peers, line_peers = others("row_0", "row_1"), others("col", "half")
+    line_peers = others("col", "half")
     barrier = pltpu.get_barrier_semaphore()
-    for peer in plane_peers + line_peers:
+    beside = [{"col": lax.rem(z + step, 8)} for step in (1, 7)]
+    near = others("row_0") + others("row_1") + beside + others("half")
+    for peer in near:
         pl.semaphore_signal(barrier, inc=1, device_id=peer, device_id_type=MESH)
     loads[0].wait()
     loads[1].wait()
@@ -328,10 +330,16 @@
         operators=operators, second=second, first=first, middles=(middle0, middle1), volume=volume,
     )
     group(0)
-    pl.semaphore_wait(barrier, 30)
-    gathered[half, z, in_plane] = info_ref[...]
+    pl.semaphore_wait(barrier, len(near))
+
+    def relay(index, peers):
+        for peer in peers:
+            pl.semaphore_signal(relay_sem.at[index], inc=1, device_id=peer, device_id_type=MESH)
+
+    relay(0, beside)
+    gathered[half, z, x, y] = info_ref[...]
     info_copies = exchange(
-        plane_peers, lambda peer: info_ref, gathered.at[half, z, in_plane], small_send.at[0], small_recv.at[0]
+        others("row_0"), lambda peer: info_ref, gathered.at[half, z, x, y], small_send.at[0], small_recv.at[0]
     )
     pending = list(info_copies)
     for ring in flat:
@@ -339,12 +347,23 @@
     group(1)
     for ring in flat:
         ring.send_right()
+    pl.semaphore_wait(relay_sem.at[0], 2)
+    relay(1, beside)
     group(2)
     for ring in flat:
         ring.send_left()
+    pl.semaphore_wait(relay_sem.at[1], 2)
+    relay(2, beside)
     group(3)
+    arrived(info_copies)
+    column = gathered.at[half, z, :, y]
+    info_copies = exchange(others("row_1"), lambda peer: column, column, small_send.at[2], small_recv.at[2])
+    pending += info_copies
+    pl.semaphore_wait(relay_sem.at[2], 2)
+    relay(3, others("half"))
     for ring in flat:
         ring.forward()
+    pl.semaphore_wait(relay_sem.at[3], 1)
     arrived(info_copies)
     info_copies = exchange(
         line_peers, lambda peer: gathered.at[half, z], gathered.at[half, z], small_send.at[1], small_recv.at[1]
@@ -486,7 +505,7 @@
             f32(2, 2, GRID, 128),
             f32(2, 8, 2, 8, 128),
             pltpu.VMEM((1, 128), jnp.int32),
-            pltpu.VMEM((2, 8, 16, 1, 128), jnp.int32),
+            pltpu.VMEM((2, 8, 4, 4, 1, 128), jnp.int32),
             f32(2, 2, 8, 128),
             f32(2, 2, 8, 128),
             f32(2, 8, 128),
@@ -505,6 +524,7 @@
             dma((5, 16)),
             dma((5, 16)),
             dma((2,)),
+            pltpu.SemaphoreType.REGULAR((4,)),
         ],
         compiler_params=pltpu.CompilerParams(
             collective_id=0, has_side_effects=True, vmem_limit_bytes=60 * 2**20

time: 42.9 us -> 42.2 us (0.984)
  Pallas kernels: 42.1 us -> 41.4 us
    pallas_call x1, Pallas kernels: 41.5 us -> 40.8 us  [local(): pl.pallas_call(kernel, out_shape=tuple((pltpu.VMEM(shape.shape, F32) for...]
where the time goes in v7:
time: 42.2 us; the launch traced here: 42.1 us
  Pallas kernels  41.4 us (98%)
  between operations  0.64 us (2%)
    pallas_call x1, Pallas kernels, local(): pl.pallas_call(kernel, out_shape=tuple((pltpu.VMEM(shape.shape, F32) for...  40.8 us

profile of v7, /device:TPU:1, one launch (start us, length us, event | category | flops | bytes accessed | tf_op | source)
XLA Modules:
  0.0 42.1 jit_solution(10658784224191637263)
XLA Ops:
  0.6 40.8 %halfmaps.1 = (f32[1,2,4,512]{3,2,1,0:T(4,128)S(1)}, f32[2,29]{1,0:T(2,128)S(1)}, f32[1,29]{1,0:T(1,128)S(1)}) custom-call(bf16[2,2,64,4096]{3,2,1,0:T(8,128)(2,1)} %particle_hbm.1, s32[2]{0:T(128)} %bin_hbm.1, s32[2,2]{1,0:T(2,128)} %slope_hbm.1, bf16[16,3,64,64]{3,2,1,0:T(8,128)(2,1)} %table_hbm.1), custom_call_target="tpu_custom_call" | custom-call | tf_op jit(solution)/shard_map/halfmaps/pallas_call | solution.py:488
  41.4 0.6 %emit.1 = (f32[1,2,4,512]{3,2,1,0:T(4,128)}, f32[2,29]{1,0:T(2,128)}, f32[1,29]{1,0:T(1,128)}) custom-call(f32[1,2,4,512]{3,2,1,0:T(4,128)S(1)} %get-tuple-element.6.map_ref, f32[2,29]{1,0:T(2,128)S(1)} %get-tuple-element.7.power_ref, f32[1,29]{1,0:T(1,128)S(1)} %get-tuple-element.8.correlation_ref), custom_call_target="tpu_custom_call" | custom-call | tf_op jit(solution)/shard_map/emit/pallas_call | solution.py:534

commit v8 on v7

--- a/solution.py
+++ b/solution.py
@@ -33,23 +33,24 @@
     return (plane == iota((GRID, GRID), 1)).astype(F32).astype(BF16)
 
 
-def along_first(particle, order, bins, slopes, data, table, first):
+def wedge(particle, slopes):
     wave_first = iota((GRID, 128), 0) - 32
     wave_third = (iota((GRID, 128), 1) & 63) - 32
     limit = jnp.where(wave_first * wave_third >= 0, slopes[particle, 0], slopes[particle, 1])
-    inside = 16 * jnp.abs(wave_third) <= limit * jnp.abs(wave_first)
-    weight = inside.astype(F32).astype(BF16)
-    kernel = jnp.dot(order, table[bins[particle], 0], preferred_element_type=F32).astype(BF16)
-
+    return (16 * jnp.abs(wave_third) <= limit * jnp.abs(wave_first)).astype(F32).astype(BF16)
+
+
+def along_first(particle, begin, end, rows, kernel, weight, data, first):
     def pairs(step, carry):
         for inner in range(16):
-            pair = step * 16 + inner
+            pair = begin + step * 16 + inner
             columns = pl.ds(pl.multiple_of(pair * 128, 128), 128)
             both = jnp.concatenate([data[particle, part, :, columns] * weight for part in range(2)], axis=1)
-            first[particle, pair] = jnp.dot(kernel, both, preferred_element_type=F32).astype(BF16)
+            lines = jnp.dot(kernel, both, preferred_element_type=F32)
+            first[particle, pair, rows, :] = lines.astype(BF16)
         return carry
 
-    lax.fori_loop(0, 2, pairs, 0)
+    lax.fori_loop(0, (end - begin) // 16, pairs, 0)
 
 
 def third_operator(kernel):
@@ -278,8 +279,11 @@
                 (bin_hbm, bins),
                 (slope_hbm, slopes),
                 (table_hbm, table),
-                (particle_hbm.at[0], data.at[0]),
-                (particle_hbm.at[1], data.at[1]),
+            )
+            + tuple(
+                (particle_hbm.at[particle, :, :, pl.ds(start, 2048)], data.at[particle, :, :, pl.ds(start, 2048)])
+                for particle in range(2)
+                for start in (0, 2048)
             )
         )
     ]
@@ -307,9 +311,16 @@
     second = jnp.concatenate(
         [table[bins[particle], 1].astype(F32) for particle in range(2)], axis=1
     ).astype(BF16)
+    weights = [wedge(particle, slopes) for particle in range(2)]
+    kernels = [
+        jnp.dot(order, table[bins[particle], 0], preferred_element_type=F32).astype(BF16) for particle in range(2)
+    ]
     for particle in range(2):
-        loads[3 + particle].wait()
-        along_first(particle, order, bins, slopes, data, table, first)
+        for side in range(2):
+            loads[3 + 2 * particle + side].wait()
+            along_first(
+                particle, 16 * side, 16 * side + 16, pl.ds(0, 16), kernels[particle][:16], weights[particle], data, first
+            )
 
     rings = [
         [
@@ -344,6 +355,8 @@
     pending = list(info_copies)
     for ring in flat:
         ring.send_far()
+    for particle in range(2):
+        along_first(particle, 0, 32, pl.ds(16, 48), kernels[particle][16:], weights[particle], data, first)
     group(1)
     for ring in flat:
         ring.send_right()
@@ -514,7 +527,7 @@
             f32((GRID + 1) * 2 * BINS, 128),
             f32(2, BINS, GRID, 128),
             f32(GRID, 128),
-            dma((5,)),
+            dma((7,)),
             dma((2, 2, 6)),
             dma((2, 2, 6)),
             dma((2, 2, 4)),

time: 42.2 us -> 41.5 us (0.983)
  Pallas kernels: 41.4 us -> 40.7 us
    pallas_call x1, Pallas kernels: 40.8 us -> 40.1 us  [local(): pl.pallas_call(kernel, out_shape=tuple((pltpu.VMEM(shape.shape, F32) for...]
where the time goes in v8:
time: 41.5 us; the launch traced here: 41.4 us
  Pallas kernels  40.7 us (98%)
  between operations  0.64 us (2%)
    pallas_call x1, Pallas kernels, local(): pl.pallas_call(kernel, out_shape=tuple((pltpu.VMEM(shape.shape, F32) for...  40.1 us

profile of v8, /device:TPU:1, one launch (start us, length us, event | category | flops | bytes accessed | tf_op | source)
XLA Modules:
  0.0 41.4 jit_solution(992669093198067409)
XLA Ops:
  0.6 40.1 %halfmaps.1 = (f32[1,2,4,512]{3,2,1,0:T(4,128)S(1)}, f32[2,29]{1,0:T(2,128)S(1)}, f32[1,29]{1,0:T(1,128)S(1)}) custom-call(bf16[2,2,64,4096]{3,2,1,0:T(8,128)(2,1)} %particle_hbm.1, s32[2]{0:T(128)} %bin_hbm.1, s32[2,2]{1,0:T(2,128)} %slope_hbm.1, bf16[16,3,64,64]{3,2,1,0:T(8,128)(2,1)} %table_hbm.1), custom_call_target="tpu_custom_call" | custom-call | tf_op jit(solution)/shard_map/halfmaps/pallas_call | solution.py:501
  40.7 0.6 %emit.1 = (f32[1,2,4,512]{3,2,1,0:T(4,128)}, f32[2,29]{1,0:T(2,128)}, f32[1,29]{1,0:T(1,128)}) custom-call(f32[1,2,4,512]{3,2,1,0:T(4,128)S(1)} %get-tuple-element.6.map_ref, f32[2,29]{1,0:T(2,128)S(1)} %get-tuple-element.7.power_ref, f32[1,29]{1,0:T(1,128)S(1)} %get-tuple-element.8.correlation_ref), custom_call_target="tpu_custom_call" | custom-call | tf_op jit(solution)/shard_map/emit/pallas_call | solution.py:547
